TPU v7x, 128 devices: a whole 4x4x4 slice. The times are simulated.
128 devices in a mesh: lat: 8 (over x, core), lon: 16 (over z, y).
Axes of the slice: x: 4, y: 4, z: 4, core: 2. Of those that a mesh axis runs over, the one named last changes fastest.
Arguments:
- grid_latent: bfloat16 [32, 2048, 512], P('lat', 'lon'), may hold values from -6 to 6
- mesh_latent: bfloat16 [16384, 512], P(('lat', 'lon')), may hold values from -6 to 6
- g2m_edges: bfloat16 [262144, 512], P(('lat', 'lon')), may hold values from -6 to 6
- g2m_senders: int32 [128, 2048], P(('lat', 'lon')), may hold values from 0 to 1631, as said below
- g2m_receivers: int32 [128, 2048], P(('lat', 'lon')), may hold values from 0 to 127, as said below
- mm_edges: bfloat16 [262144, 512], P(('lat', 'lon')), may hold values from -6 to 6
- mm_senders: int32 [128, 2048], P(('lat', 'lon')), may hold values from 0 to 2175
- mm_receivers: int32 [128, 2048], P(('lat', 'lon')), may hold values from 0 to 128, as said below
- send_rows: int32 [128, 2048], P(('lat', 'lon')), may hold values from 0 to 127
- edge_in: bfloat16 [3, 3, 512, 512], replicated, may hold values from -0.15625 to 0.15625
- edge_out: bfloat16 [3, 512, 512], replicated, may hold values from -0.25 to 0.25
- node_in: bfloat16 [3, 2, 512, 512], replicated, may hold values from -0.1875 to 0.1875
- node_out: bfloat16 [3, 512, 512], replicated, may hold values from -0.25 to 0.25
- norm_gain: float32 [3, 2, 512], replicated, may hold values from 0.5 to 1.5
- norm_bias: float32 [3, 2, 512], replicated, may hold values from -1.5 to 1.5
Outputs:
- mesh_out: bfloat16 [16384, 512], P(('lat', 'lon'))
Inputs may be any that keep to these rules, and one draw needn't show every extreme that they name: `g2m_receivers`: each patch's edges are sorted by receiver; every mesh node of a patch receives at least one grid-to-mesh edge; the sender cell lies within 4 rows and columns of a cell that is fixed for the receiving node. `g2m_senders`: A flat index into the tile extended by 4 cells, with rows of 136 cells. `mm_receivers`: sorted within a patch; the used slots come first and the unused ones hold 128; some patch uses all 2048 slots in every draw.
All inputs are finite; a program needn't handle non-finite values.
Results may differ from a plain program's by a relative error of at most 0.012.
Values may be sent and summed in bfloat16 or wider, within the bound.
No kernel may reach another device: no remote copies, remote signals or barrier semaphores. Data moves between devices by JAX's collectives and lax.ppermute only.
A program may use at most 128 MiB of HBM per device.

v0:
```python
import math

import jax
import jax.numpy as jnp
from jax import lax
from jax.sharding import PartitionSpec as P

HALO = 4


NORM_EPS = 1e-05


def padded_2(array, sides, width, wrap):
    for axis, dim in sides:
        size, length = (lax.axis_size(axis), array.shape[dim])
        up = [(i, (i + 1) % size) for i in range(size if wrap else size - 1)]
        down = [(j, i) for i, j in up]
        last = lax.slice_in_dim(array, length - width, length, axis=dim)
        leading = lax.slice_in_dim(array, 0, width, axis=dim)
        before = lax.ppermute(last, axis, up)
        after = lax.ppermute(leading, axis, down)
        array = jnp.concatenate([before, array, after], axis=dim)
    return array


def normalize(values, gains, biases):
    centre = jnp.mean(values, axis=-1, keepdims=True)
    spread = jnp.mean(jnp.square(values - centre), axis=-1, keepdims=True)
    return (values - centre) * lax.rsqrt(spread + NORM_EPS) * gains + biases


def project(values, weights):
    return jnp.dot(values, weights, preferred_element_type=jnp.float32).astype(jnp.bfloat16)


def edge_update(edge_rows, sender_terms, receiver_terms, weights_in, weights_out, gains, biases):
    pre_act = jnp.dot(edge_rows, weights_in, preferred_element_type=jnp.float32)
    pre_act = pre_act + sender_terms.astype(jnp.float32) + receiver_terms.astype(jnp.float32)
    hidden = jax.nn.silu(pre_act).astype(jnp.bfloat16)
    output = jnp.dot(hidden, weights_out, preferred_element_type=jnp.float32)
    return (edge_rows.astype(jnp.float32) + normalize(output, gains, biases)).astype(jnp.bfloat16)


def node_update(nodes, summed, weights_in, weights_out, gains, biases):
    pre_act = jnp.dot(nodes, weights_in[0], preferred_element_type=jnp.float32)
    pre_act = pre_act + jnp.dot(
        summed.astype(jnp.bfloat16), weights_in[1], preferred_element_type=jnp.float32
    )
    hidden = jax.nn.silu(pre_act).astype(jnp.bfloat16)
    output = jnp.dot(hidden, weights_out, preferred_element_type=jnp.float32)
    return (nodes.astype(jnp.float32) + normalize(output, gains, biases)).astype(jnp.bfloat16)


def pick_rows(table, indices):
    count = indices.shape[0]
    block_rows = math.gcd(count, 512)
    table_rows = jnp.arange(table.shape[0], dtype=jnp.int32)

    def one_block(piece):
        selector = (piece[:, None] == table_rows[None, :]).astype(table.dtype)
        return jnp.dot(selector, table, preferred_element_type=jnp.float32).astype(table.dtype)

    picked = lax.map(one_block, indices.reshape(-1, block_rows))
    return picked.reshape(count, table.shape[1])


def incidence_sum(edge_rows, receivers, node_count):
    incidence = (jnp.arange(node_count, dtype=jnp.int32)[:, None] == receivers[None, :]).astype(
        jnp.bfloat16
    )
    return jnp.dot(incidence, edge_rows, preferred_element_type=jnp.float32)


def local(
    grid_latent,
    mesh_latent,
    g2m_edges,
    g2m_senders,
    g2m_receivers,
    mm_edges,
    mm_senders,
    mm_receivers,
    send_rows,
    edge_in,
    edge_out,
    node_in,
    node_out,
    norm_gain,
    norm_bias,
):
    features = grid_latent.shape[-1]
    node_count = mesh_latent.shape[0]
    operand = project(grid_latent.reshape(-1, features), edge_in[0, 1]).reshape(grid_latent.shape)
    widened = padded_2(operand, (("lon", 1),), HALO, True)
    padded = padded_2(widened, (("lat", 0),), HALO, False)
    flat_tile = padded.reshape(-1, features)
    sent = pick_rows(flat_tile, g2m_senders[0])
    receiver_table = project(mesh_latent, edge_in[0, 2])
    got = pick_rows(receiver_table, g2m_receivers[0])
    encoded = edge_update(
        g2m_edges, sent, got, edge_in[0, 0], edge_out[0], norm_gain[0, 0], norm_bias[0, 0]
    )
    summed = incidence_sum(encoded, g2m_receivers[0], node_count)
    mesh_nodes = node_update(
        mesh_latent, summed, node_in[0], node_out[0], norm_gain[0, 1], norm_bias[0, 1]
    )
    receivers = mm_receivers[0]
    clipped = jnp.minimum(receivers, node_count - 1)
    edge_state = mm_edges
    for level in range(1, edge_in.shape[0]):
        outgoing = project(mesh_nodes, edge_in[level, 1])
        out_rows = pick_rows(outgoing, send_rows[0])
        arrived = lax.all_to_all(out_rows, ("lat", "lon"), split_axis=0, concat_axis=0, tiled=True)
        combined = jnp.concatenate([outgoing, arrived], axis=0)
        sent = pick_rows(combined, mm_senders[0])
        recv_table = project(mesh_nodes, edge_in[level, 2])
        got = pick_rows(recv_table, clipped)
        edge_state = edge_update(
            edge_state,
            sent,
            got,
            edge_in[level, 0],
            edge_out[level],
            norm_gain[level, 0],
            norm_bias[level, 0],
        )
        summed = incidence_sum(edge_state, receivers, node_count)
        mesh_nodes = node_update(
            mesh_nodes,
            summed,
            node_in[level],
            node_out[level],
            norm_gain[level, 1],
            norm_bias[level, 1],
        )
    return mesh_nodes


def solution(mesh):
    in_specs = (
        P("lat", "lon", None),
        P(("lat", "lon"), None),
        P(("lat", "lon"), None),
        P(("lat", "lon"), None),
        P(("lat", "lon"), None),
        P(("lat", "lon"), None),
        P(("lat", "lon"), None),
        P(("lat", "lon"), None),
        P(("lat", "lon"), None),
        P(),
        P(),
        P(),
        P(),
        P(),
        P(),
    )
    out_specs = P(("lat", "lon"), None)
    return jax.shard_map(local, mesh=mesh, in_specs=in_specs, out_specs=out_specs, check_vma=False)
```

profile of v0, /device:TPU:0, one launch (start us, length us, event | category | flops | bytes accessed | tf_op | source)
XLA Modules:
  0.0 206.7 jit_solution(11114943986987234662)
XLA Ops:
  1.0 1.5 convolution_convert_fusion.5
  2.5 1.8 collective-permute-start
  4.3 5.0 %collective-permute-start.1 = (bf16[4,4,512]{2,1,0:T(4,128)(2,1)S(1)}, bf16[4,4,512]{2,1,0:T(4,128)(2,1)S(1)}, u32[]{:S(2)}, u32[]{:S(2)}) collective-permute-start(bf16[4,4,512]{2,1,0:T(4,128)(2,1)S(1)} %get-tuple-element.374), channel_id=1, source_target_pairs={{1,0},{2,1},{3,2},{4,3},{5,4},{6,5},{7,6},{8,7},{9,8},{10,9},{11,1... | collective-permute-start | bytes 49160 | tf_op jit(solution)/shard_map/ppermute | solution.py:22
  12.6 1.5 while.89
  15.2 2.4 %collective-permute-start.2 = (bf16[4,136,512]{2,1,0:T(8,128)(2,1)}, bf16[4,136,512]{2,1,0:T(8,128)(2,1)}, u32[]{:S(2)}, u32[]{:S(2)}) collective-permute-start(bf16[4,136,512]{2,1,0:T(8,128)(2,1)} %pad_maximum_fusion.3), channel_id=1, source_target_pairs={{0,16},{16,32},{32,48},{48,64},{64,80},{80,96},{96,112},{1,17},{17... | collective-permute-start | bytes 1671176 | tf_op jit(solution)/shard_map/ppermute | solution.py:21
  19.5 3.9 %copy.16 = bf16[2048,512]{0,1:T(8,128)(2,1)} copy(bf16[2048,512]{1,0:T(8,128)(2,1)} %param.33) | data formatting | bytes 4194304 | tf_op args[2]
  25.4 2.6 %pad_maximum_fusion.2 = bf16[12,136,512]{2,1,0:T(8,128)(2,1)} fusion(bf16[4,136,512]{2,1,0:T(8,128)(2,1)} %collective-permute-done.3, bf16[4,4,512]{2,1,0:T(4,128)(2,1)S(1)} %collective-permute-done.1, bf16[4,128,512]{2,1,0:T(8,128)(2,1)S(1)} %bitcast.242, bf16[4,4,512]{2,1,0:T(4,128)(2,1)S(1)} %collective-permute-done, ...), kind=kLoop, calls=%fused_computation.78 | loop fusion | flops 8355840 | bytes 3342336 | tf_op jit(solution)/shard_map/concatenate | solution.py:23
  28.0 1.5 broadcast.136.clone.1
  29.5 13.7 %while.88 = (s32[]{:T(128)}, bf16[4,512,512]{2,1,0:T(8,128)(2,1)}, s32[4,512]{1,0:T(4,128)S(1)}, bf16[1632,512]{1,0:T(8,128)(2,1)}, s32[]{:T(128)}) while((s32[]{:T(128)}, bf16[4,512,512]{2,1,0:T(8,128)(2,1)}, s32[4,512]{1,0:T(4,128)S(1)}, bf16[1632,512]{1,0:T(8,128)(2,1)}, s32[]{:T(128)}) %tuple.174), condition=%wide.region_1.2_spmd.clone, body=%wide.region_0.1_spmd.clone.sunk | while | flops 856735744 | bytes 2202177 | solution.py:64
  29.5 3.4 %fusion.178 = bf16[4,512,512]{2,1,0:T(8,128)(2,1)} fusion(bf16[4,512,512]{2,1,0:T(8,128)(2,1)} %get-tuple-element.620, s32[]{:T(128)} %get-tuple-element.619, bf16[1632,512]{1,0:T(8,128)(2,1)} %get-tuple-element.627, s32[512]{0:T(512)S(1)} %bitcast.255), kind=kOutput, calls=%fused_computation.13.clone.1 | convolution fusion | flops 856735744 | bytes 2198016 | tf_op jit(solution)/shard_map/while/body/eval_jaxpr/dot_general | solution.py:62
  32.9 3.4 %fusion.178 = bf16[4,512,512]{2,1,0:T(8,128)(2,1)} fusion(bf16[4,512,512]{2,1,0:T(8,128)(2,1)} %get-tuple-element.620, s32[]{:T(128)} %get-tuple-element.619, bf16[1632,512]{1,0:T(8,128)(2,1)} %get-tuple-element.627, s32[512]{0:T(512)S(1)} %bitcast.255), kind=kOutput, calls=%fused_computation.13.clone.1 | convolution fusion | flops 856735744 | bytes 2198016 | tf_op jit(solution)/shard_map/while/body/eval_jaxpr/dot_general | solution.py:62
  36.4 3.4 %fusion.178 = bf16[4,512,512]{2,1,0:T(8,128)(2,1)} fusion(bf16[4,512,512]{2,1,0:T(8,128)(2,1)} %get-tuple-element.620, s32[]{:T(128)} %get-tuple-element.619, bf16[1632,512]{1,0:T(8,128)(2,1)} %get-tuple-element.627, s32[512]{0:T(512)S(1)} %bitcast.255), kind=kOutput, calls=%fused_computation.13.clone.1 | convolution fusion | flops 856735744 | bytes 2198016 | tf_op jit(solution)/shard_map/while/body/eval_jaxpr/dot_general | solution.py:62
  39.8 3.4 %fusion.178 = bf16[4,512,512]{2,1,0:T(8,128)(2,1)} fusion(bf16[4,512,512]{2,1,0:T(8,128)(2,1)} %get-tuple-element.620, s32[]{:T(128)} %get-tuple-element.619, bf16[1632,512]{1,0:T(8,128)(2,1)} %get-tuple-element.627, s32[512]{0:T(512)S(1)} %bitcast.255), kind=kOutput, calls=%fused_computation.13.clone.1 | convolution fusion | flops 856735744 | bytes 2198016 | tf_op jit(solution)/shard_map/while/body/eval_jaxpr/dot_general | solution.py:62
  43.2 7.3 %fusion.125 = (f32[2048]{0:T(1024)S(1)}, f32[2048,512]{0,1:T(8,128)}) fusion(bf16[3,512,512]{2,1,0:T(8,128)(2,1)} %param.41, bf16[2048,512]{1,0:T(8,128)(2,1)S(1)} %bitcast.244, bf16[2048,512]{1,0:T(8,128)(2,1)} %bitcast.245, bf16[2048,512]{1,0:T(8,128)(2,1)} %param.33, bf16[3,3,512,512]{3,2,1,0:T(8,128)(2,1)} %param.40), kind=kOutput, calls=%fused_computation.176 | convolution fusion | flops 2157967360 | bytes 11542528 | tf_op jit(solution)/shard_map/dot_general | solution.py:41
  50.5 2.8 %multiply_reduce_fusion.2 = f32[2048]{0:T(1024)S(1)} fusion(f32[2048,512]{0,1:T(8,128)} %get-tuple-element.388, f32[2048]{0:T(1024)S(1)} %broadcast_multiply_fusion.2), kind=kLoop, calls=%fused_computation.72 | loop fusion | flops 3143680 | bytes 4210688 | tf_op jit(solution)/shard_map/reduce_sum | solution.py:29
  53.4 3.8 %multiply_convert_fusion.5 = bf16[128,512]{1,0:T(8,128)(2,1)S(1)} fusion(f32[128,512]{1,0:T(8,128)S(1)} %fusion.81, bf16[3,2,512,512]{3,2,1,0:T(8,128)(2,1)} %param.42, bf16[2048,512]{0,1:T(8,128)(2,1)S(1)} %copy-done.7, f32[2048,512]{0,1:T(8,128)} %get-tuple-element.388, f32[512]{0:T(512)S(1)} %bitcast.272, f32[512]{0:T(512)S(1)} %bitcast.271, ...), kind=kOutput, calls=%fused_computation.156 | convolution fusion | flops 343605248 | bytes 7237632 | tf_op jit(solution)/shard_map/dot_general | solution.py:47
  60.3 1.5 while.90
  63.2 10.6 %all-to-all-start = ((bf16[128,16,512]{2,1,0:T(8,128)(2,1)}), bf16[128,16,512]{2,1,0:T(8,128)(2,1)S(1)}, u32[]{:S(2)}, u32[]{:S(2)}) async-start(bf16[128,16,512]{2,1,0:T(8,128)(2,1)} %bitcast.238), calls=%async_computation | async-start | bytes 4194304 | tf_op jit(solution)/shard_map/all_to_all | solution.py:114
  74.5 3.9 %copy.17 = bf16[2048,512]{0,1:T(8,128)(2,1)} copy(bf16[2048,512]{1,0:T(8,128)(2,1)} %param.36) | data formatting | bytes 4194304 | tf_op args[5]
  81.0 1.5 broadcast.136.clone.2
  82.5 4.7 %while.92 = (s32[]{:T(128)}, bf16[4,512,512]{2,1,0:T(8,128)(2,1)}, s32[4,512]{1,0:T(4,128)S(1)}, bf16[128,512]{1,0:T(8,128)(2,1)S(1)}, s32[]{:T(128)}) while((s32[]{:T(128)}, bf16[4,512,512]{2,1,0:T(8,128)(2,1)}, s32[4,512]{1,0:T(4,128)S(1)}, bf16[128,512]{1,0:T(8,128)(2,1)S(1)}, s32[]{:T(128)}) %tuple.156), condition=%wide.region_13.14_spmd.clone, body=%wide.region_12.13_spmd.clone.sunk | while | flops 67436544 | bytes 662081 | solution.py:64
  87.2 16.3 %all-to-all-done = bf16[128,16,512]{2,1,0:T(8,128)(2,1)S(1)} async-done(((bf16[128,16,512]{2,1,0:T(8,128)(2,1)}), bf16[128,16,512]{2,1,0:T(8,128)(2,1)S(1)}, u32[]{:S(2)}, u32[]{:S(2)}) %all-to-all-start) | async-done | bytes 2097184 | tf_op jit(solution)/shard_map/all_to_all | solution.py:114
  103.4 1.5 pad_maximum_fusion
  105.1 12.4 %while.91 = (s32[]{:T(128)}, bf16[4,512,512]{2,1,0:T(8,128)(2,1)S(1)}, s32[4,512]{1,0:T(4,128)S(1)}, bf16[2176,512]{1,0:T(8,128)(2,1)}, s32[]{:T(128)}) while((s32[]{:T(128)}, bf16[4,512,512]{2,1,0:T(8,128)(2,1)S(1)}, s32[4,512]{1,0:T(4,128)S(1)}, bf16[2176,512]{1,0:T(8,128)(2,1)}, s32[]{:T(128)}) %tuple.162), condition=%wide.region_11.12_spmd.clone, body=%wide.region_10.11_spmd.clone.sunk | while | flops 1142226944 | bytes 2758725 | solution.py:64
  105.1 3.1 %fusion.184 = bf16[4,512,512]{2,1,0:T(8,128)(2,1)S(1)} fusion(bf16[4,512,512]{2,1,0:T(8,128)(2,1)S(1)} %get-tuple-element.665, s32[]{:T(128)} %get-tuple-element.664, bf16[2176,512]{1,0:T(8,128)(2,1)} %get-tuple-element.672, s32[512]{0:T(512)S(1)} %bitcast.256), kind=kOutput, calls=%fused_computation.32.clone.1 | convolution fusion | flops 1142226944 | bytes 2754564 | tf_op jit(solution)/shard_map/while/body/eval_jaxpr/dot_general | solution.py:62
  108.2 3.1 %fusion.184 = bf16[4,512,512]{2,1,0:T(8,128)(2,1)S(1)} fusion(bf16[4,512,512]{2,1,0:T(8,128)(2,1)S(1)} %get-tuple-element.665, s32[]{:T(128)} %get-tuple-element.664, bf16[2176,512]{1,0:T(8,128)(2,1)} %get-tuple-element.672, s32[512]{0:T(512)S(1)} %bitcast.256), kind=kOutput, calls=%fused_computation.32.clone.1 | convolution fusion | flops 1142226944 | bytes 2754564 | tf_op jit(solution)/shard_map/while/body/eval_jaxpr/dot_general | solution.py:62
  111.3 3.1 %fusion.184 = bf16[4,512,512]{2,1,0:T(8,128)(2,1)S(1)} fusion(bf16[4,512,512]{2,1,0:T(8,128)(2,1)S(1)} %get-tuple-element.665, s32[]{:T(128)} %get-tuple-element.664, bf16[2176,512]{1,0:T(8,128)(2,1)} %get-tuple-element.672, s32[512]{0:T(512)S(1)} %bitcast.256), kind=kOutput, calls=%fused_computation.32.clone.1 | convolution fusion | flops 1142226944 | bytes 2754564 | tf_op jit(solution)/shard_map/while/body/eval_jaxpr/dot_general | solution.py:62
  114.4 3.1 %fusion.184 = bf16[4,512,512]{2,1,0:T(8,128)(2,1)S(1)} fusion(bf16[4,512,512]{2,1,0:T(8,128)(2,1)S(1)} %get-tuple-element.665, s32[]{:T(128)} %get-tuple-element.664, bf16[2176,512]{1,0:T(8,128)(2,1)} %get-tuple-element.672, s32[512]{0:T(512)S(1)} %bitcast.256), kind=kOutput, calls=%fused_computation.32.clone.1 | convolution fusion | flops 1142226944 | bytes 2754564 | tf_op jit(solution)/shard_map/while/body/eval_jaxpr/dot_general | solution.py:62
  117.5 1.4 copy-done.6
  118.9 8.1 %fusion.129 = (f32[2048]{0:T(1024)S(1)}, f32[2048,512]{0,1:T(8,128)}) fusion(bf16[3,512,512]{2,1,0:T(8,128)(2,1)} %param.41, bf16[2048,512]{1,0:T(8,128)(2,1)} %bitcast.246, bf16[2048,512]{1,0:T(8,128)(2,1)} %bitcast.247, bf16[2048,512]{1,0:T(8,128)(2,1)} %param.36, bf16[3,3,512,512]{3,2,1,0:T(8,128)(2,1)} %param.40), kind=kOutput, calls=%fused_computation.178 | convolution fusion | flops 2157967360 | bytes 11542528 | tf_op jit(solution)/shard_map/dot_general | solution.py:41
  127.0 2.8 %multiply_reduce_fusion.1 = f32[2048]{0:T(1024)S(1)} fusion(f32[2048,512]{0,1:T(8,128)} %get-tuple-element.392, f32[2048]{0:T(1024)S(1)} %broadcast_multiply_fusion.1), kind=kLoop, calls=%fused_computation.69 | loop fusion | flops 3143680 | bytes 4210688 | tf_op jit(solution)/shard_map/reduce_sum | solution.py:29
  130.4 2.4 %add_convert_fusion.1 = bf16[2048,512]{0,1:T(8,128)(2,1)} fusion(bf16[2048,512]{0,1:T(8,128)(2,1)S(1)} %copy-done.5, f32[2048,512]{0,1:T(8,128)S(1)} %copy-done.2, f32[512]{0:T(512)S(1)} %bitcast.268, f32[512]{0:T(512)S(1)} %bitcast.267, f32[2048]{0:T(1024)S(1)} %add_rsqrt_fusion.1, f32[2048]{0:T(1024)S(1)} %broadcast_multiply_fusion.1), kind=kLoop, calls=%fused_computation.68 | loop fusion | flops 7340032 | bytes 8409088 | tf_op jit(solution)/shard_map/convert_element_type | solution.py:42
  132.8 2.7 %multiply_convert_fusion.4 = bf16[128,512]{1,0:T(8,128)(2,1)S(1)} fusion(f32[128,512]{1,0:T(8,128)S(1)} %fusion.71, bf16[3,2,512,512]{3,2,1,0:T(8,128)(2,1)} %param.42, bf16[2048,512]{0,1:T(8,128)(2,1)} %add_convert_fusion.1, s32[2048]{0:T(1024)S(1)} %bitcast.265), kind=kOutput, calls=%fused_computation.153 | convolution fusion | flops 336265216 | bytes 3022848 | tf_op jit(solution)/shard_map/dot_general | solution.py:47
  135.5 1.4 fusion.132
  138.6 1.5 while.93
  141.5 4.9 %all-to-all-start.1 = ((bf16[128,16,512]{2,1,0:T(8,128)(2,1)}), bf16[128,16,512]{2,1,0:T(8,128)(2,1)S(1)}, u32[]{:S(2)}, u32[]{:S(2)}) async-start(bf16[128,16,512]{2,1,0:T(8,128)(2,1)} %bitcast.239), calls=%async_computation.1 | async-start | bytes 4194304 | tf_op jit(solution)/shard_map/all_to_all | solution.py:114
  149.0 1.5 broadcast.136.clone.5
  150.5 4.7 %while.95 = (s32[]{:T(128)}, bf16[4,512,512]{2,1,0:T(8,128)(2,1)}, s32[4,512]{1,0:T(4,128)S(1)}, bf16[128,512]{1,0:T(8,128)(2,1)S(1)}, s32[]{:T(128)}) while((s32[]{:T(128)}, bf16[4,512,512]{2,1,0:T(8,128)(2,1)}, s32[4,512]{1,0:T(4,128)S(1)}, bf16[128,512]{1,0:T(8,128)(2,1)S(1)}, s32[]{:T(128)}) %tuple.177), condition=%wide.region_23.24_spmd.clone, body=%wide.region_22.23_spmd.clone.sunk | while | flops 67436544 | bytes 662081 | solution.py:64
  155.1 20.8 %all-to-all-done.1 = bf16[128,16,512]{2,1,0:T(8,128)(2,1)S(1)} async-done(((bf16[128,16,512]{2,1,0:T(8,128)(2,1)}), bf16[128,16,512]{2,1,0:T(8,128)(2,1)S(1)}, u32[]{:S(2)}, u32[]{:S(2)}) %all-to-all-start.1) | async-done | bytes 2097184 | tf_op jit(solution)/shard_map/all_to_all | solution.py:114
  176.0 1.5 pad_maximum_fusion.1
  177.7 12.4 %while.94 = (s32[]{:T(128)}, bf16[4,512,512]{2,1,0:T(8,128)(2,1)S(1)}, s32[4,512]{1,0:T(4,128)S(1)}, bf16[2176,512]{1,0:T(8,128)(2,1)}, s32[]{:T(128)}) while((s32[]{:T(128)}, bf16[4,512,512]{2,1,0:T(8,128)(2,1)S(1)}, s32[4,512]{1,0:T(4,128)S(1)}, bf16[2176,512]{1,0:T(8,128)(2,1)}, s32[]{:T(128)}) %tuple.176), condition=%wide.region_21.22_spmd.clone, body=%wide.region_20.21_spmd.clone.sunk | while | flops 1142226944 | bytes 2758725 | solution.py:64
  177.7 3.1 %fusion.190 = bf16[4,512,512]{2,1,0:T(8,128)(2,1)S(1)} fusion(bf16[4,512,512]{2,1,0:T(8,128)(2,1)S(1)} %get-tuple-element.710, s32[]{:T(128)} %get-tuple-element.709, bf16[2176,512]{1,0:T(8,128)(2,1)} %get-tuple-element.717, s32[512]{0:T(512)S(1)} %bitcast.257), kind=kOutput, calls=%fused_computation.51.clone.1 | convolution fusion | flops 1142226944 | bytes 2754564 | tf_op jit(solution)/shard_map/while/body/eval_jaxpr/dot_general | solution.py:62
  180.8 3.1 %fusion.190 = bf16[4,512,512]{2,1,0:T(8,128)(2,1)S(1)} fusion(bf16[4,512,512]{2,1,0:T(8,128)(2,1)S(1)} %get-tuple-element.710, s32[]{:T(128)} %get-tuple-element.709, bf16[2176,512]{1,0:T(8,128)(2,1)} %get-tuple-element.717, s32[512]{0:T(512)S(1)} %bitcast.257), kind=kOutput, calls=%fused_computation.51.clone.1 | convolution fusion | flops 1142226944 | bytes 2754564 | tf_op jit(solution)/shard_map/while/body/eval_jaxpr/dot_general | solution.py:62
  183.9 3.1 %fusion.190 = bf16[4,512,512]{2,1,0:T(8,128)(2,1)S(1)} fusion(bf16[4,512,512]{2,1,0:T(8,128)(2,1)S(1)} %get-tuple-element.710, s32[]{:T(128)} %get-tuple-element.709, bf16[2176,512]{1,0:T(8,128)(2,1)} %get-tuple-element.717, s32[512]{0:T(512)S(1)} %bitcast.257), kind=kOutput, calls=%fused_computation.51.clone.1 | convolution fusion | flops 1142226944 | bytes 2754564 | tf_op jit(solution)/shard_map/while/body/eval_jaxpr/dot_general | solution.py:62
  187.0 3.1 %fusion.190 = bf16[4,512,512]{2,1,0:T(8,128)(2,1)S(1)} fusion(bf16[4,512,512]{2,1,0:T(8,128)(2,1)S(1)} %get-tuple-element.710, s32[]{:T(128)} %get-tuple-element.709, bf16[2176,512]{1,0:T(8,128)(2,1)} %get-tuple-element.717, s32[512]{0:T(512)S(1)} %bitcast.257), kind=kOutput, calls=%fused_computation.51.clone.1 | convolution fusion | flops 1142226944 | bytes 2754564 | tf_op jit(solution)/shard_map/while/body/eval_jaxpr/dot_general | solution.py:62
  190.1 7.6 %fusion.133 = (f32[2048]{0:T(1024)S(1)}, f32[2048,512]{0,1:T(8,128)}) fusion(bf16[3,512,512]{2,1,0:T(8,128)(2,1)} %param.41, bf16[2048,512]{1,0:T(8,128)(2,1)} %bitcast.248, bf16[2048,512]{1,0:T(8,128)(2,1)S(1)} %bitcast.243, bf16[2048,512]{0,1:T(8,128)(2,1)} %add_convert_fusion.1, bf16[3,3,512,512]{3,2,1,0:T(8,128)(2,1)} %param.40), kind=kOutput, calls=%fused_computation.180 | convolution fusion | flops 2157967360 | bytes 11542528 | tf_op jit(solution)/shard_map/dot_general | solution.py:41
  197.6 2.8 %multiply_reduce_fusion = f32[2048]{0:T(1024)S(1)} fusion(f32[2048,512]{0,1:T(8,128)} %get-tuple-element.396, f32[2048]{0:T(1024)S(1)} %broadcast_multiply_fusion), kind=kLoop, calls=%fused_computation.66 | loop fusion | flops 3143680 | bytes 4210688 | tf_op jit(solution)/shard_map/reduce_sum | solution.py:29
  200.5 3.8 %multiply_convert_fusion.3 = bf16[128,512]{1,0:T(8,128)(2,1)S(1)} fusion(f32[128,512]{1,0:T(8,128)S(1)} %fusion.61, bf16[3,2,512,512]{3,2,1,0:T(8,128)(2,1)} %param.42, bf16[2048,512]{0,1:T(8,128)(2,1)S(1)} %copy-done.8, f32[2048,512]{0,1:T(8,128)} %get-tuple-element.396, f32[512]{0:T(512)S(1)} %bitcast.270, f32[512]{0:T(512)S(1)} %bitcast.269, ...), kind=kOutput, calls=%fused_computation.150 | convolution fusion | flops 343605248 | bytes 7237632 | tf_op jit(solution)/shard_map/dot_general | solution.py:47
  (138 shorter events, 39.5 us)
Async XLA Ops:
  0.0 1.0 copy-start
  2.5 11.6 %collective-permute-start = (bf16[4,4,512]{2,1,0:T(4,128)(2,1)S(1)}, bf16[4,4,512]{2,1,0:T(4,128)(2,1)S(1)}, u32[]{:S(2)}, u32[]{:S(2)}) collective-permute-start(bf16[4,4,512]{2,1,0:T(4,128)(2,1)S(1)} %get-tuple-element.373), channel_id=1, source_target_pairs={{0,1},{1,2},{2,3},{3,4},{4,5},{5,6},{6,7},{7,8},{8,9},{9,10},{10,1... | collective-permute-start | bytes 49160 | tf_op jit(solution)/shard_map/ppermute | solution.py:21
  4.3 9.9 %collective-permute-start.1 = (bf16[4,4,512]{2,1,0:T(4,128)(2,1)S(1)}, bf16[4,4,512]{2,1,0:T(4,128)(2,1)S(1)}, u32[]{:S(2)}, u32[]{:S(2)}) collective-permute-start(bf16[4,4,512]{2,1,0:T(4,128)(2,1)S(1)} %get-tuple-element.374), channel_id=1, source_target_pairs={{1,0},{2,1},{3,2},{4,3},{5,4},{6,5},{7,6},{8,7},{9,8},{10,9},{11,1... | collective-permute-start | bytes 49160 | tf_op jit(solution)/shard_map/ppermute | solution.py:22
  12.6 6.3 %copy-start.10 = (f32[3,2,512]{2,1,0:T(2,128)S(1)}, f32[3,2,512]{2,1,0:T(2,128)}, u32[]{:S(2)}) copy-start(f32[3,2,512]{2,1,0:T(2,128)} %param.44) | copy-start | bytes 36868
  12.6 6.3 %copy-start.12 = (s32[1,2048]{1,0:T(1,128)S(1)}, s32[1,2048]{1,0:T(1,128)}, u32[]{:S(2)}) copy-start(s32[1,2048]{1,0:T(1,128)} %param.34) | copy-start | bytes 24580
  15.2 8.3 %copy-start.13 = (s32[1,2048]{1,0:T(1,128)S(1)}, s32[1,2048]{1,0:T(1,128)}, u32[]{:S(2)}) copy-start(s32[1,2048]{1,0:T(1,128)} %param.39) | copy-start | bytes 24580
  15.2 8.9 %copy-start.11 = (f32[3,2,512]{2,1,0:T(2,128)S(1)}, f32[3,2,512]{2,1,0:T(2,128)}, u32[]{:S(2)}) copy-start(f32[3,2,512]{2,1,0:T(2,128)} %param.45) | copy-start | bytes 36868
  15.2 8.9 %copy-start.9 = (bf16[128,512]{1,0:T(8,128)(2,1)S(1)}, bf16[128,512]{1,0:T(8,128)(2,1)}, u32[]{:S(2)}) copy-start(bf16[128,512]{1,0:T(8,128)(2,1)} %param.32) | copy-start | bytes 393220
  15.2 10.2 %collective-permute-start.2 = (bf16[4,136,512]{2,1,0:T(8,128)(2,1)}, bf16[4,136,512]{2,1,0:T(8,128)(2,1)}, u32[]{:S(2)}, u32[]{:S(2)}) collective-permute-start(bf16[4,136,512]{2,1,0:T(8,128)(2,1)} %pad_maximum_fusion.3), channel_id=1, source_target_pairs={{0,16},{16,32},{32,48},{48,64},{64,80},{80,96},{96,112},{1,17},{17... | collective-permute-start | bytes 1671176 | tf_op jit(solution)/shard_map/ppermute | solution.py:21
  17.6 7.8 %collective-permute-start.3 = (bf16[4,136,512]{2,1,0:T(8,128)(2,1)}, bf16[4,136,512]{2,1,0:T(8,128)(2,1)}, u32[]{:S(2)}, u32[]{:S(2)}) collective-permute-start(bf16[4,136,512]{2,1,0:T(8,128)(2,1)} %pad_maximum_fusion.3), channel_id=1, source_target_pairs={{16,0},{32,16},{48,32},{64,48},{80,64},{96,80},{112,96},{17,1},{33... | collective-permute-start | bytes 1671176 | tf_op jit(solution)/shard_map/ppermute | solution.py:22
  50.5 2.9 %copy-start.7 = (bf16[2048,512]{0,1:T(8,128)(2,1)S(1)}, bf16[2048,512]{0,1:T(8,128)(2,1)}, u32[]{:S(2)}) copy-start(bf16[2048,512]{0,1:T(8,128)(2,1)} %copy.16) | copy-start | bytes 6291460
  50.5 2.9 %copy-start.14 = (s32[1,2048]{1,0:T(1,128)S(1)}, s32[1,2048]{1,0:T(1,128)}, u32[]{:S(2)}) copy-start(s32[1,2048]{1,0:T(1,128)} %param.35) | copy-start | bytes 24580
  61.8 1.4 copy-start.3
  61.8 12.0 %copy-start.15 = (s32[1,2048]{1,0:T(1,128)S(1)}, s32[1,2048]{1,0:T(1,128)}, u32[]{:S(2)}) copy-start(s32[1,2048]{1,0:T(1,128)} %param.37) | copy-start | bytes 24580
  61.8 12.6 %copy-start.16 = (s32[1,2048]{1,0:T(1,128)S(1)}, s32[1,2048]{1,0:T(1,128)}, u32[]{:S(2)}) copy-start(s32[1,2048]{1,0:T(1,128)} %param.38) | copy-start | bytes 24580
  63.2 40.2 %all-to-all-start = ((bf16[128,16,512]{2,1,0:T(8,128)(2,1)}), bf16[128,16,512]{2,1,0:T(8,128)(2,1)S(1)}, u32[]{:S(2)}, u32[]{:S(2)}) async-start(bf16[128,16,512]{2,1,0:T(8,128)(2,1)} %bitcast.238), calls=%async_computation | async-start | bytes 4194304 | tf_op jit(solution)/shard_map/all_to_all | solution.py:114
  117.5 1.4 copy-start.6
  118.9 10.9 %copy-start.5 = (bf16[2048,512]{0,1:T(8,128)(2,1)S(1)}, bf16[2048,512]{0,1:T(8,128)(2,1)}, u32[]{:S(2)}) copy-start(bf16[2048,512]{0,1:T(8,128)(2,1)} %copy.17) | copy-start | bytes 6291460
  127.0 3.4 %copy-start.2 = (f32[2048,512]{0,1:T(8,128)S(1)}, f32[2048,512]{0,1:T(8,128)}, u32[]{:S(2)}) copy-start(f32[2048,512]{0,1:T(8,128)} %get-tuple-element.392) | copy-start | bytes 12582916
  140.2 1.4 copy-start.4
  141.5 34.4 %all-to-all-start.1 = ((bf16[128,16,512]{2,1,0:T(8,128)(2,1)}), bf16[128,16,512]{2,1,0:T(8,128)(2,1)S(1)}, u32[]{:S(2)}, u32[]{:S(2)}) async-start(bf16[128,16,512]{2,1,0:T(8,128)(2,1)} %bitcast.239), calls=%async_computation.1 | async-start | bytes 4194304 | tf_op jit(solution)/shard_map/all_to_all | solution.py:114
  197.6 2.9 %copy-start.8 = (bf16[2048,512]{0,1:T(8,128)(2,1)S(1)}, bf16[2048,512]{0,1:T(8,128)(2,1)}, u32[]{:S(2)}) copy-start(bf16[2048,512]{0,1:T(8,128)(2,1)} %add_convert_fusion.1) | copy-start | bytes 6291460
  200.5 6.2 %copy-start.1 = (bf16[4,128,512]{2,1,0:T(8,128)(2,1)S(1)}, bf16[4,128,512]{2,1,0:T(8,128)(2,1)}, u32[]{:S(2)}) copy-start(bf16[4,128,512]{2,1,0:T(8,128)(2,1)} %param.31) | copy-start | bytes 1572868
where the time goes:
time: 208 us; the launch traced here: 207 us
  matrix products  101 us (49%)
  waiting for transfers between devices  37.1 us (18%)
  starting transfers between devices  25.9 us (12%)
  other arithmetic  22.2 us (11%)
  local copies, waits for them, and re-layouts  19.9 us (10%)
    dot_general x32, matrix products, one_block(): jnp.dot(selector, table, preferred_element_type=jnp.float32)  51.5 us
    all_to_all x2, waiting for transfers between devices, local(): lax.all_to_all(out_rows, ('lat', 'lon'), split_axis=0, concat_axis=0, til...  37.1 us
    dot_general x3, matrix products, edge_update(): output = jnp.dot(hidden, weights_out, preferred_element_type=jnp.float32)  23 us
    all_to_all x2, starting transfers between devices, local(): lax.all_to_all(out_rows, ('lat', 'lon'), split_axis=0, concat_axis=0, til...  15.5 us
    unnamed x37, local copies, waits for them, and re-layouts  14.2 us
    dot_general x3, matrix products, node_update(): jnp.dot(summed.astype(jnp.bfloat16), weights_in[1], preferred_element_typ...  10.3 us
    reduce_sum x6, other arithmetic, normalize(): spread = jnp.mean(jnp.square(values - centre), axis=-1, keepdims=True)  8.91 us
    dot_general x6, matrix products, project(): jnp.dot(values, weights, preferred_element_type=jnp.float32)  7.9 us
  transfers between devices with their start and end apart: 6, of which 2 were waited for; matrix products, arithmetic and copies ran while one was open for 16% of the time, Pallas kernels for 0%

commit v1 on v0

v1 whole, which is shorter than its diff:
```python
import functools

import jax
import jax.numpy as jnp
from jax import lax
from jax.experimental import pallas as pl
from jax.experimental.pallas import tpu as pltpu
from jax.sharding import PartitionSpec as P

HALO = 4
NORM_EPS = 1e-05
F32 = jnp.float32
BF16 = jnp.bfloat16
BLOCK = 256
GROUP = 16
MIB = 1024 * 1024


def silu(values):
    half = values * 0.5
    return half + half * jnp.tanh(half)


def normalize(values, gains, biases):
    centre = jnp.mean(values, axis=-1, keepdims=True)
    shifted = values - centre
    spread = jnp.mean(shifted * shifted, axis=-1, keepdims=True)
    return shifted * lax.rsqrt(spread + NORM_EPS) * gains + biases


def dot(left, right):
    return jnp.dot(left, right, preferred_element_type=F32)


def project(values, weights):
    return dot(values, weights).astype(BF16)


def hot_columns(indices, nodes):
    places = lax.broadcasted_iota(jnp.int32, (nodes, indices.shape[1]), 0)
    return jnp.where(places == indices, 1.0, 0.0).astype(BF16)


def hot_rows(indices, nodes):
    places = lax.broadcasted_iota(jnp.int32, (nodes, indices.shape[1]), 0)
    return jnp.where(places == indices, 1.0, 0.0).T.astype(BF16)


def pre_kernel(extra, edges, receivers, nodes, w_edge, w_recv, *refs):
    if extra:
        tile, w_send, send_rows, pre, tile_terms, picks = refs
    else:
        (pre,) = refs
    node_count = nodes.shape[0]
    terms = project(nodes[...], w_recv[...])
    edge_count = edges.shape[0]

    def step(i, _):
        at = pl.multiple_of(i * BLOCK, BLOCK)
        rows = pl.ds(at, BLOCK)
        hot = hot_rows(jnp.minimum(receivers[:, rows], node_count - 1), node_count)
        pre[rows, :] = dot(edges[rows, :], w_edge[...]) + dot(hot, terms)
        if extra:
            picks[rows, :] = hot_rows(send_rows[:, rows], node_count)
        return 0

    lax.fori_loop(0, edge_count // BLOCK, step, 0)
    if extra:
        tile_terms[...] = project(tile[...], w_send[...])


def main_kernel(pieces, last, keep, senders, receivers, pre, edges, w_out, edge_norm, nodes,
                w_node, w_node_out, node_norm, *refs):
    refs = list(refs)
    tables = [refs.pop(0) for _ in range(pieces)]
    w_send = refs.pop(0) if pieces > 2 else None
    if not last:
        w_next, picks = refs.pop(0), refs.pop(0)
    new_nodes = refs.pop(0)
    if not last:
        outgoing, out_rows = refs.pop(0), refs.pop(0)
    new_edges = refs.pop(0) if keep else None
    table, hidden, total = refs
    node_count = nodes.shape[0]
    edge_count = edges.shape[0]

    start = 0
    for index, piece in enumerate(tables):
        size = piece.shape[0]
        if w_send is not None and index > 0:
            values = project(piece[...], w_send[...]).astype(F32)
        else:
            values = piece[...].astype(F32)
        table[start:start + size, :] = values
        start += size

    total[...] = jnp.zeros_like(total)
    sublane = lax.broadcasted_iota(jnp.int32, (8, table.shape[1]), 0)

    def step(i, _):
        at = pl.multiple_of(i * BLOCK, BLOCK)
        rows = pl.ds(at, BLOCK)
        for group in range(BLOCK // GROUP):
            parts = []
            for half in range(GROUP // 8):
                first = group * GROUP + half * 8
                gathered = None
                for j in range(8):
                    row = senders[at + (first + j)]
                    value = jnp.broadcast_to(table[pl.ds(row, 1), :], sublane.shape)
                    gathered = value if j == 0 else jnp.where(sublane == j, value, gathered)
                begin = pl.multiple_of(at + first, 8)
                parts.append(silu(pre[pl.ds(begin, 8), :] + gathered))
            hidden[group * GROUP:(group + 1) * GROUP, :] = jnp.concatenate(parts, 0).astype(BF16)
        output = dot(hidden[...], w_out[...])
        fresh = edges[rows, :].astype(F32) + normalize(output, edge_norm[0:1, :], edge_norm[1:2, :])
        fresh = fresh.astype(BF16)
        if keep:
            new_edges[rows, :] = fresh
        total[...] += dot(hot_columns(receivers[:, rows], node_count), fresh)
        return 0

    lax.fori_loop(0, edge_count // BLOCK, step, 0)

    here = nodes[...]
    pre_node = dot(here, w_node[0]) + dot(total[...].astype(BF16), w_node[1])
    output = dot(silu(pre_node).astype(BF16), w_node_out[...])
    updated = here.astype(F32) + normalize(output, node_norm[0:1, :], node_norm[1:2, :])
    updated = updated.astype(BF16)
    new_nodes[...] = updated
    if not last:
        sent = project(updated, w_next[...])
        outgoing[...] = sent

        def pick(i, _):
            rows = pl.ds(pl.multiple_of(i * BLOCK, BLOCK), BLOCK)
            out_rows[rows, :] = dot(picks[rows, :], sent).astype(BF16)
            return 0

        lax.fori_loop(0, picks.shape[0] // BLOCK, pick, 0)


VMEM = pl.BlockSpec(memory_space=pltpu.VMEM)
SMEM = pl.BlockSpec(memory_space=pltpu.SMEM)


def pre_stage(edges, receivers, nodes, w_edge, w_recv, extra=()):
    edge_count, width = edges.shape
    node_count = nodes.shape[0]
    out_shape = [jax.ShapeDtypeStruct((edge_count, width), F32)]
    if extra:
        out_shape += [
            jax.ShapeDtypeStruct(extra[0].shape, BF16),
            jax.ShapeDtypeStruct((extra[2].shape[1], node_count), BF16),
        ]
    operands = (edges, receivers, nodes, w_edge, w_recv, *extra)
    return pl.pallas_call(
        functools.partial(pre_kernel, bool(extra)),
        out_shape=out_shape,
        in_specs=[VMEM] * len(operands),
        out_specs=[VMEM] * len(out_shape),
        name="pre_first" if extra else "pre_next",
        cost_estimate=pl.CostEstimate(
            flops=2 * edge_count * width * (width + node_count),
            bytes_accessed=edge_count * width * 6,
            transcendentals=0,
        ),
        compiler_params=pltpu.CompilerParams(vmem_limit_bytes=24 * MIB),
    )(*operands)


def main_stage(senders, receivers, pre, edges, w_out, edge_norm, nodes, w_node, w_node_out,
               node_norm, tables, w_send, following, keep, name):
    edge_count, width = edges.shape
    node_count = nodes.shape[0]
    operands = [senders, receivers, pre, edges, w_out, edge_norm, nodes, w_node, w_node_out,
                node_norm, *tables]
    if w_send is not None:
        operands.append(w_send)
    out_shape = []
    out_shape.append(jax.ShapeDtypeStruct((node_count, width), BF16))
    if following is not None:
        operands += list(following)
        out_shape.append(jax.ShapeDtypeStruct((node_count, width), BF16))
        out_shape.append(jax.ShapeDtypeStruct((following[1].shape[0], width), BF16))
    if keep:
        out_shape.append(jax.ShapeDtypeStruct((edge_count, width), BF16))
    table_rows = sum(piece.shape[0] for piece in tables)
    return pl.pallas_call(
        functools.partial(main_kernel, len(tables), following is None, keep),
        out_shape=out_shape,
        in_specs=[SMEM] + [VMEM] * (len(operands) - 1),
        out_specs=[VMEM] * len(out_shape),
        scratch_shapes=[
            pltpu.VMEM((table_rows, width), F32),
            pltpu.VMEM((BLOCK, width), BF16),
            pltpu.VMEM((node_count, width), F32),
        ],
        name=name,
        cost_estimate=pl.CostEstimate(
            flops=2 * edge_count * width * (width + node_count),
            bytes_accessed=edge_count * width * 10,
            transcendentals=edge_count * width,
        ),
        compiler_params=pltpu.CompilerParams(vmem_limit_bytes=32 * MIB),
    )(*operands)


def shift(array, axis, step, wrap):
    size = lax.axis_size(axis)
    pairs = [(i, (i + step) % size) for i in range(size) if wrap or 0 <= i + step < size]
    return lax.ppermute(array, axis, pairs)


def local(
    grid_latent,
    mesh_latent,
    g2m_edges,
    g2m_senders,
    g2m_receivers,
    mm_edges,
    mm_senders,
    mm_receivers,
    send_rows,
    edge_in,
    edge_out,
    node_in,
    node_out,
    norm_gain,
    norm_bias,
):
    high, wide, features = grid_latent.shape
    norms = jnp.stack([norm_gain, norm_bias], axis=2)

    west = shift(grid_latent[:, wide - HALO:, :], "lon", 1, True)
    east = shift(grid_latent[:, :HALO, :], "lon", -1, True)
    north = shift(grid_latent, "lat", 1, False)
    south = shift(grid_latent, "lat", -1, False)
    sides = jnp.concatenate([west, east], axis=1)
    north_sides = shift(sides, "lat", 1, False)
    south_sides = shift(sides, "lat", -1, False)

    tile_width = wide + 2 * HALO
    cell = g2m_senders[0]
    row, column = cell // tile_width, cell % tile_width
    band = jnp.where(row < HALO, 1, jnp.where(row < HALO + high, 0, 2))
    inner = row - jnp.where(band == 1, 0, jnp.where(band == 0, HALO, HALO + high))
    tile_cells = high * wide
    side_width = 2 * HALO
    side = jnp.where(column < HALO, column, column - wide)
    inside = jnp.logical_and(column >= HALO, column < HALO + wide)
    places = jnp.where(
        inside,
        band * tile_cells + inner * wide + column - HALO,
        3 * tile_cells + (band * high + inner) * side_width + side,
    )

    flat_tile = grid_latent.reshape(tile_cells, features)
    pre, tile_terms, picks = pre_stage(
        g2m_edges, g2m_receivers, mesh_latent, edge_in[0, 0], edge_in[0, 2],
        (flat_tile, edge_in[0, 1], send_rows),
    )
    all_sides = jnp.concatenate([sides, north_sides, south_sides], axis=0)
    tables = [
        tile_terms,
        north.reshape(tile_cells, features),
        south.reshape(tile_cells, features),
        all_sides.reshape(-1, features),
    ]
    nodes, outgoing, out_rows = main_stage(
        places, g2m_receivers, pre, g2m_edges, edge_out[0], norms[0, 0], mesh_latent, node_in[0],
        node_out[0], norms[0, 1], tables, edge_in[0, 1], (edge_in[1, 1], picks), False, "encode",
    )
    edges = mm_edges
    levels = edge_in.shape[0]
    for level in range(1, levels):
        devices = lax.axis_size("lat") * lax.axis_size("lon")
        blocks = out_rows.reshape(devices, -1, features)
        arrived = lax.all_to_all(blocks, ("lat", "lon"), split_axis=0, concat_axis=0, tiled=True)
        arrived = arrived.reshape(-1, features)
        (pre,) = pre_stage(edges, mm_receivers, nodes, edge_in[level, 0], edge_in[level, 2])
        final = level == levels - 1
        following = None if final else (edge_in[level + 1, 1], picks)
        results = main_stage(
            mm_senders[0], mm_receivers, pre, edges, edge_out[level], norms[level, 0], nodes,
            node_in[level], node_out[level], norms[level, 1], [outgoing, arrived], None, following,
            not final, "layer",
        )
        if final:
            (nodes,) = results
        else:
            nodes, outgoing, out_rows, edges = results
    return nodes


def solution(mesh):
    in_specs = (
        P("lat", "lon", None),
        P(("lat", "lon"), None),
        P(("lat", "lon"), None),
        P(("lat", "lon"), None),
        P(("lat", "lon"), None),
        P(("lat", "lon"), None),
        P(("lat", "lon"), None),
        P(("lat", "lon"), None),
        P(("lat", "lon"), None),
        P(),
        P(),
        P(),
        P(),
        P(),
        P(),
    )
    out_specs = P(("lat", "lon"), None)
    return jax.shard_map(local, mesh=mesh, in_specs=in_specs, out_specs=out_specs, check_vma=False)
```

time: 208 us -> 167 us (0.80)
  matrix products: 101 us -> 0 us
  Pallas kernels: 0 us -> 52.2 us
  other arithmetic: 22.2 us -> 2.15 us
  local copies, waits for them, and re-layouts: 19.9 us -> 35.5 us
  waiting for transfers between devices: 37.1 us -> 43.7 us
  starting transfers between devices: 25.9 us -> 31.6 us
    dot_general x50 -> x0, matrix products: 101 us -> none  [the longest x32 51.5 us: one_block(): jnp.dot(selector, table, preferred_element_type=jnp.float32)]
    pallas_call x0 -> x6, Pallas kernels: none -> 52.2 us  [the longest x3 41.2 us: main_stage(): pl.pallas_call(functools.partial(main_kernel, len(tables), following is N...]
    unnamed x37 -> x78, local copies, waits for them, and re-layouts: 14.2 us -> 28.3 us
    reduce_sum x6 -> x0, other arithmetic: 8.91 us -> none  [normalize(): spread = jnp.mean(jnp.square(values - centre), axis=-1, keepdims=True)]
    concatenate x4 -> x1, other arithmetic: 6.63 us -> 0.02 us  [local(): sides = jnp.concatenate([west, east], axis=1)]
    squeeze x0 -> x3, local copies, waits for them, and re-layouts: none -> 6.38 us  [the longest x1 3.35 us: local(): node_in[level]]
    all_to_all x2, waiting for transfers between devices: 37.1 us -> 43.5 us  [local(): lax.all_to_all(blocks, ('lat', 'lon'), split_axis=0, concat_axis=0, tiled...]
    another operation x12 -> x2, local copies, waits for them, and re-layouts: 5.36 us -> 0.02 us  [local(): norms = jnp.stack([norm_gain, norm_bias], axis=2)]
  transfers between devices with their start and end apart: 6 -> 8, of which waited for: 2 -> 3; matrix products, arithmetic and copies ran while one was open for 16% -> 6% of each run, Pallas kernels for 0% -> 7%
where the time goes in v1:
time: 167 us; the launch traced here: 165 us
  Pallas kernels  52.2 us (31%)
  waiting for transfers between devices  43.7 us (26%)
  local copies, waits for them, and re-layouts  35.5 us (21%)
  starting transfers between devices  31.6 us (19%)
  other arithmetic  2.15 us (1%)
    all_to_all x2, waiting for transfers between devices, local(): lax.all_to_all(blocks, ('lat', 'lon'), split_axis=0, concat_axis=0, tiled...  43.5 us
    pallas_call x3, Pallas kernels, main_stage(): pl.pallas_call(functools.partial(main_kernel, len(tables), following is N...  41.2 us
    unnamed x78, local copies, waits for them, and re-layouts  28.3 us
    all_to_all x2, starting transfers between devices, local(): lax.all_to_all(blocks, ('lat', 'lon'), split_axis=0, concat_axis=0, tiled...  15.9 us
    ppermute x6, starting transfers between devices, shift(): return lax.ppermute(array, axis, pairs)  15.7 us
    pallas_call x3, Pallas kernels, pre_stage(): pl.pallas_call(functools.partial(pre_kernel, bool(extra)), out_shape=out_...  11 us
    squeeze x1, local copies, waits for them, and re-layouts, local(): node_in[level]  3.35 us
  transfers between devices with their start and end apart: 8, of which 3 were waited for; matrix products, arithmetic and copies ran while one was open for 6% of the time, Pallas kernels for 7%

profile of v1, /device:TPU:0, one launch (start us, length us, event | category | flops | bytes accessed | tf_op | source)
XLA Modules:
  0.0 165.5 jit_solution(11439478447990596222)
XLA Ops:
  0.0 1.3 collective-permute-start
  1.3 1.3 collective-permute-start.1
  2.6 0.8 fusion.15
  3.4 2.2 %collective-permute-start.2 = (bf16[4,4,512]{2,1,0:T(4,128)(2,1)S(1)}, bf16[4,4,512]{2,1,0:T(4,128)(2,1)S(1)}, u32[]{:S(2)}, u32[]{:S(2)}) collective-permute-start(bf16[4,4,512]{2,1,0:T(4,128)(2,1)S(1)} %get-tuple-element.43), channel_id=1, source_target_pairs={{0,1},{1,2},{2,3},{3,4},{4,5},{5,6},{6,7},{7,8},{8,9},{9,10},{10,1... | collective-permute-start | bytes 49160 | tf_op jit(solution)/shard_map/ppermute | solution.py:212
  5.6 5.0 %collective-permute-start.3 = (bf16[4,4,512]{2,1,0:T(4,128)(2,1)S(1)}, bf16[4,4,512]{2,1,0:T(4,128)(2,1)S(1)}, u32[]{:S(2)}, u32[]{:S(2)}) collective-permute-start(bf16[4,4,512]{2,1,0:T(4,128)(2,1)S(1)} %get-tuple-element.44), channel_id=1, source_target_pairs={{0,15},{1,0},{2,1},{3,2},{4,3},{5,4},{6,5},{7,6},{8,7},{9,8},{10,9... | collective-permute-start | bytes 49160 | tf_op jit(solution)/shard_map/ppermute | solution.py:212
  10.6 0.7 compare_reduce_fusion
  11.4 0.7 broadcast_remainder_fusion
  12.1 3.4 %slice_bitcast_fusion = (bf16[2,512,512]{2,1,0:T(8,128)(2,1)S(1)}, bf16[2,512,512]{2,1,0:T(8,128)(2,1)S(1)}, bf16[2,512,512]{2,1,0:T(8,128)(2,1)}) fusion(bf16[3,2,512,512]{3,2,1,0:T(8,128)(2,1)} %param.26), kind=kLoop, calls=%fused_computation | loop fusion | bytes 6291456 | tf_op jit(solution)/shard_map/squeeze | solution.py:286
  15.5 1.6 slice_bitcast_fusion.5
  17.0 0.8 copy-done.35
  17.8 0.5 copy-done.36
  18.3 1.5 slice_bitcast_fusion.3
  19.8 0.9 copy-done.8
  20.8 4.0 %pre_first.1 = (f32[2048,512]{1,0:T(8,128)S(1)}, bf16[512,512]{1,0:T(8,128)(2,1)S(1)}, bf16[2048,128]{1,0:T(8,128)(2,1)S(1)}) custom-call(bf16[2048,512]{1,0:T(8,128)(2,1)S(1)} %copy-done.8, s32[1,2048]{1,0:T(1,128)S(1)} %copy-done.31, bf16[128,512]{1,0:T(8,128)(2,1)S(1)} %copy-done.22, bf16[512,512]{1,0:T(8,128)(2,1)S(1)} %get-tuple-element.32.w_edge, ...), custom_call_target="tpu_custom_call" | custom-call | flops 1342177280 | bytes 6291456 | tf_op jit(solution)/shard_map/pre_first/pallas_call | solution.py:157
  24.9 1.3 collective-permute-start.5
  26.2 4.6 %collective-permute-start.4 = (bf16[4,8,512]{2,1,0:T(8,128)(2,1)S(1)}, bf16[4,8,512]{2,1,0:T(8,128)(2,1)S(1)}, u32[]{:S(2)}, u32[]{:S(2)}) collective-permute-start(bf16[4,8,512]{2,1,0:T(8,128)(2,1)S(1)} %pad_maximum_fusion), channel_id=1, source_target_pairs={{0,16},{16,32},{32,48},{48,64},{64,80},{80,96},{96,112},{1,17},{17... | collective-permute-start | bytes 98312 | tf_op jit(solution)/shard_map/ppermute | solution.py:212
  30.8 0.6 fusion.9
  31.4 0.2 collective-permute-done.4
  31.7 13.9 %encode.1 = (bf16[128,512]{1,0:T(8,128)(2,1)S(1)}, bf16[128,512]{1,0:T(8,128)(2,1)S(1)}, bf16[2048,512]{1,0:T(8,128)(2,1)S(1)}) custom-call(s32[2048]{0:T(1024)S(1)} %fusion.1.senders, s32[1,2048]{1,0:T(1,128)S(1)} %copy-done.31, f32[2048,512]{1,0:T(8,128)S(1)} %get-tuple-element.15.pre, bf16[2048,512]{1,0:T(8,128)(2,1)S(1)} %copy-done.8, ...), custom_call_target="tpu_custom_call" | custom-call | flops 1342177280 | bytes 10485760 | tf_op jit(solution)/shard_map/encode/pallas_call | solution.py:189
  45.6 1.4 copy-done.20
  47.0 10.0 %all-to-all-start = ((bf16[128,16,512]{2,1,0:T(8,128)(2,1)}), bf16[128,16,512]{2,1,0:T(8,128)(2,1)}, u32[]{:S(2)}, u32[]{:S(2)}) async-start(bf16[128,16,512]{2,1,0:T(8,128)(2,1)} %bitcast.60), calls=%async_computation | async-start | bytes 4194304 | tf_op jit(solution)/shard_map/all_to_all | solution.py:279
  57.0 1.0 copy-done.16
  58.0 1.0 copy-done.17
  59.1 3.5 %pre_next.2.pre = f32[2048,512]{1,0:T(8,128)S(1)} custom-call(bf16[2048,512]{1,0:T(8,128)(2,1)S(1)} %copy-done.4, s32[1,2048]{1,0:T(1,128)S(1)} %copy-done.25, bf16[128,512]{1,0:T(8,128)(2,1)S(1)} %get-tuple-element.18.nodes, bf16[512,512]{1,0:T(8,128)(2,1)S(1)} %copy-done.17, bf16[512,512]{1,0:T(8,128)(2,1)S(1)} %copy-done.16), custom_call_target="tpu_custom_call" | custom-call | flops 1342177280 | bytes 6291456 | tf_op jit(solution)/shard_map/pre_next/pallas_call | solution.py:157
  62.6 2.0 %copy-done = f32[2048,512]{1,0:T(8,128)} copy-done((f32[2048,512]{1,0:T(8,128)}, f32[2048,512]{1,0:T(8,128)S(1)}, u32[]{:S(2)}) %copy-start) | copy-done | bytes 4194328
  64.6 21.7 %all-to-all-done = bf16[128,16,512]{2,1,0:T(8,128)(2,1)} async-done(((bf16[128,16,512]{2,1,0:T(8,128)(2,1)}), bf16[128,16,512]{2,1,0:T(8,128)(2,1)}, u32[]{:S(2)}, u32[]{:S(2)}) %all-to-all-start) | async-done | bytes 2097184 | tf_op jit(solution)/shard_map/all_to_all | solution.py:279
  86.3 2.2 %copy-done.1 = f32[2048,512]{1,0:T(8,128)S(1)} copy-done((f32[2048,512]{1,0:T(8,128)S(1)}, f32[2048,512]{1,0:T(8,128)}, u32[]{:S(2)}) %copy-start.1) | copy-done | bytes 4194328
  88.5 1.2 copy-done.7
  89.7 1.0 copy-done.13
  90.8 1.0 copy-done.14
  91.8 1.0 copy-done.15
  92.9 1.0 copy-done.19
  93.9 0.7 copy-done.27
  94.6 0.7 copy-done.28
  95.3 14.2 %layer.2 = (bf16[128,512]{1,0:T(8,128)(2,1)S(1)}, bf16[128,512]{1,0:T(8,128)(2,1)S(1)}, bf16[2048,512]{1,0:T(8,128)(2,1)S(1)}, bf16[2048,512]{1,0:T(8,128)(2,1)S(1)}) custom-call(s32[2048]{0:T(1024)S(1)} %bitcast.64, s32[1,2048]{1,0:T(1,128)S(1)} %copy-done.25, f32[2048,512]{1,0:T(8,128)S(1)} %copy-done.1, bf16[2048,512]{1,0:T(8,128)(2,1)S(1)} %copy-done.4, ...), custom_call_target="tpu_custom_call" | custom-call | flops 1342177280 | bytes 10485760 | tf_op jit(solution)/shard_map/layer/pallas_call | solution.py:189
  109.5 1.3 copy-done.5
  110.8 1.4 copy-done.21
  112.2 0.7 copy-done.23
  112.9 5.9 %all-to-all-start.1 = ((bf16[128,16,512]{2,1,0:T(8,128)(2,1)}), bf16[128,16,512]{2,1,0:T(8,128)(2,1)}, u32[]{:S(2)}, u32[]{:S(2)}) async-start(bf16[128,16,512]{2,1,0:T(8,128)(2,1)} %bitcast.61), calls=%async_computation.1 | async-start | bytes 4194304 | tf_op jit(solution)/shard_map/all_to_all | solution.py:279
  118.8 1.0 copy-done.11
  119.8 1.0 copy-done.12
  120.9 3.5 %pre_next.3.pre = f32[2048,512]{1,0:T(8,128)S(1)} custom-call(bf16[2048,512]{1,0:T(8,128)(2,1)S(1)} %copy-done.6, s32[1,2048]{1,0:T(1,128)S(1)} %copy-done.25, bf16[128,512]{1,0:T(8,128)(2,1)S(1)} %get-tuple-element.22.nodes, bf16[512,512]{1,0:T(8,128)(2,1)S(1)} %copy-done.12, bf16[512,512]{1,0:T(8,128)(2,1)S(1)} %copy-done.11), custom_call_target="tpu_custom_call" | custom-call | flops 1342177280 | bytes 6291456 | tf_op jit(solution)/shard_map/pre_next/pallas_call | solution.py:157
  124.4 2.0 %copy-done.2 = f32[2048,512]{1,0:T(8,128)} copy-done((f32[2048,512]{1,0:T(8,128)}, f32[2048,512]{1,0:T(8,128)S(1)}, u32[]{:S(2)}) %copy-start.2) | copy-done | bytes 4194328
  126.4 21.7 %all-to-all-done.1 = bf16[128,16,512]{2,1,0:T(8,128)(2,1)} async-done(((bf16[128,16,512]{2,1,0:T(8,128)(2,1)}), bf16[128,16,512]{2,1,0:T(8,128)(2,1)}, u32[]{:S(2)}, u32[]{:S(2)}) %all-to-all-start.1) | async-done | bytes 2097184 | tf_op jit(solution)/shard_map/all_to_all | solution.py:279
  148.1 2.2 %copy-done.3 = f32[2048,512]{1,0:T(8,128)S(1)} copy-done((f32[2048,512]{1,0:T(8,128)S(1)}, f32[2048,512]{1,0:T(8,128)}, u32[]{:S(2)}) %copy-start.3) | copy-done | bytes 4194328
  150.3 1.0 copy-done.9
  151.4 1.0 copy-done.10
  152.4 13.1 %layer.3 = bf16[128,512]{1,0:T(8,128)(2,1)} custom-call(s32[2048]{0:T(1024)S(1)} %bitcast.65, s32[1,2048]{1,0:T(1,128)S(1)} %copy-done.25, f32[2048,512]{1,0:T(8,128)S(1)} %copy-done.3, bf16[2048,512]{1,0:T(8,128)(2,1)S(1)} %copy-done.6, bf16[512,512]{1,0:T(8,128)(2,1)S(1)} %copy-done.10, f32[2,512]{1,0:T(2,128)S(1)} %copy-done.30, ...), custom_call_target="tpu_custom_call" | custom-call | flops 1342177280 | bytes 10485760 | tf_op jit(solution)/shard_map/layer/pallas_call | solution.py:189
  (64 shorter events, 0.3 us)
Async XLA Ops:
  0.0 31.7 %collective-permute-start = (bf16[4,128,512]{2,1,0:T(8,128)(2,1)}, bf16[4,128,512]{2,1,0:T(8,128)(2,1)S(1)}, u32[]{:S(2)}, u32[]{:S(2)}) collective-permute-start(bf16[4,128,512]{2,1,0:T(8,128)(2,1)} %param.15), channel_id=1, source_target_pairs={{0,16},{16,32},{32,48},{48,64},{64,80},{80,96},{96,112},{1,17},{17... | collective-permute-start | bytes 1572872 | tf_op jit(solution)/shard_map/ppermute | solution.py:212
  1.3 30.4 %collective-permute-start.1 = (bf16[4,128,512]{2,1,0:T(8,128)(2,1)}, bf16[4,128,512]{2,1,0:T(8,128)(2,1)S(1)}, u32[]{:S(2)}, u32[]{:S(2)}) collective-permute-start(bf16[4,128,512]{2,1,0:T(8,128)(2,1)} %param.15), channel_id=1, source_target_pairs={{16,0},{32,16},{48,32},{64,48},{80,64},{96,80},{112,96},{17,1},{33... | collective-permute-start | bytes 1572872 | tf_op jit(solution)/shard_map/ppermute | solution.py:212
  3.4 21.4 %collective-permute-start.2 = (bf16[4,4,512]{2,1,0:T(4,128)(2,1)S(1)}, bf16[4,4,512]{2,1,0:T(4,128)(2,1)S(1)}, u32[]{:S(2)}, u32[]{:S(2)}) collective-permute-start(bf16[4,4,512]{2,1,0:T(4,128)(2,1)S(1)} %get-tuple-element.43), channel_id=1, source_target_pairs={{0,1},{1,2},{2,3},{3,4},{4,5},{5,6},{6,7},{7,8},{8,9},{9,10},{10,1... | collective-permute-start | bytes 49160 | tf_op jit(solution)/shard_map/ppermute | solution.py:212
  5.6 19.2 %collective-permute-start.3 = (bf16[4,4,512]{2,1,0:T(4,128)(2,1)S(1)}, bf16[4,4,512]{2,1,0:T(4,128)(2,1)S(1)}, u32[]{:S(2)}, u32[]{:S(2)}) collective-permute-start(bf16[4,4,512]{2,1,0:T(4,128)(2,1)S(1)} %get-tuple-element.44), channel_id=1, source_target_pairs={{0,15},{1,0},{2,1},{3,2},{4,3},{5,4},{6,5},{7,6},{8,7},{9,8},{10,9... | collective-permute-start | bytes 49160 | tf_op jit(solution)/shard_map/ppermute | solution.py:212
  12.1 3.4 %copy-start.34 = (bf16[3,3,512,512]{3,2,1,0:T(8,128)(2,1)S(1)}, bf16[3,3,512,512]{3,2,1,0:T(8,128)(2,1)}, u32[]{:S(2)}) copy-start(bf16[3,3,512,512]{3,2,1,0:T(8,128)(2,1)} %param.24) | copy-start | bytes 14155780
  15.5 2.4 %copy-start.35 = (bf16[3,512,512]{2,1,0:T(8,128)(2,1)S(1)}, bf16[3,512,512]{2,1,0:T(8,128)(2,1)}, u32[]{:S(2)}) copy-start(bf16[3,512,512]{2,1,0:T(8,128)(2,1)} %param.27) | copy-start | bytes 4718596
  15.5 2.8 %copy-start.36 = (bf16[3,512,512]{2,1,0:T(8,128)(2,1)S(1)}, bf16[3,512,512]{2,1,0:T(8,128)(2,1)}, u32[]{:S(2)}) copy-start(bf16[3,512,512]{2,1,0:T(8,128)(2,1)} %param.25) | copy-start | bytes 4718596
  18.3 2.3 %copy-start.8 = (bf16[2048,512]{1,0:T(8,128)(2,1)S(1)}, bf16[2048,512]{1,0:T(8,128)(2,1)}, u32[]{:S(2)}) copy-start(bf16[2048,512]{1,0:T(8,128)(2,1)} %edges.5) | copy-start | bytes 6291460
  18.3 2.3 %copy-start.22 = (bf16[128,512]{1,0:T(8,128)(2,1)S(1)}, bf16[128,512]{1,0:T(8,128)(2,1)}, u32[]{:S(2)}) copy-start(bf16[128,512]{1,0:T(8,128)(2,1)} %nodes.3) | copy-start | bytes 393220
  18.3 2.3 %copy-start.31 = (s32[1,2048]{1,0:T(1,128)S(1)}, s32[1,2048]{1,0:T(1,128)}, u32[]{:S(2)}) copy-start(s32[1,2048]{1,0:T(1,128)} %receivers.7) | copy-start | bytes 24580
  18.3 2.5 %copy-start.32 = (bf16[4,128,512]{2,1,0:T(8,128)(2,1)S(1)}, bf16[4,128,512]{2,1,0:T(8,128)(2,1)}, u32[]{:S(2)}) copy-start(bf16[4,128,512]{2,1,0:T(8,128)(2,1)} %param.15) | copy-start | bytes 1572868
  18.3 2.5 %copy-start.33 = (s32[1,2048]{1,0:T(1,128)S(1)}, s32[1,2048]{1,0:T(1,128)}, u32[]{:S(2)}) copy-start(s32[1,2048]{1,0:T(1,128)} %refs_2_.1) | copy-start | bytes 24580
  20.8 4.0 %copy-start.37 = (f32[3,2,512]{2,1,0:T(2,128)S(1)}, f32[3,2,512]{2,1,0:T(2,128)}, u32[]{:S(2)}) copy-start(f32[3,2,512]{2,1,0:T(2,128)} %param.28) | copy-start | bytes 36868
  20.8 4.0 %copy-start.38 = (f32[3,2,512]{2,1,0:T(2,128)S(1)}, f32[3,2,512]{2,1,0:T(2,128)}, u32[]{:S(2)}) copy-start(f32[3,2,512]{2,1,0:T(2,128)} %param.29) | copy-start | bytes 36868
  24.8 20.8 %copy-start.18 = (bf16[2048,128]{1,0:T(8,128)(2,1)}, bf16[2048,128]{1,0:T(8,128)(2,1)S(1)}, u32[]{:S(2)}) copy-start(bf16[2048,128]{1,0:T(8,128)(2,1)S(1)} %get-tuple-element.17.refs_6_.refs_3_) | copy-start | bytes 1572868
  24.9 6.6 %collective-permute-start.5 = (bf16[4,8,512]{2,1,0:T(8,128)(2,1)S(1)}, bf16[4,8,512]{2,1,0:T(8,128)(2,1)S(1)}, u32[]{:S(2)}, u32[]{:S(2)}) collective-permute-start(bf16[4,8,512]{2,1,0:T(8,128)(2,1)S(1)} %pad_maximum_fusion), channel_id=1, source_target_pairs={{16,0},{32,16},{48,32},{64,48},{80,64},{96,80},{112,96},{17,1},{33... | collective-permute-start | bytes 98312 | tf_op jit(solution)/shard_map/ppermute | solution.py:212
  26.2 5.5 %collective-permute-start.4 = (bf16[4,8,512]{2,1,0:T(8,128)(2,1)S(1)}, bf16[4,8,512]{2,1,0:T(8,128)(2,1)S(1)}, u32[]{:S(2)}, u32[]{:S(2)}) collective-permute-start(bf16[4,8,512]{2,1,0:T(8,128)(2,1)S(1)} %pad_maximum_fusion), channel_id=1, source_target_pairs={{0,16},{16,32},{32,48},{48,64},{64,80},{80,96},{96,112},{1,17},{17... | collective-permute-start | bytes 98312 | tf_op jit(solution)/shard_map/ppermute | solution.py:212
  45.6 1.4 copy-start.20
  47.0 10.0 %copy-start.4 = (bf16[2048,512]{1,0:T(8,128)(2,1)S(1)}, bf16[2048,512]{1,0:T(8,128)(2,1)}, u32[]{:S(2)}) copy-start(bf16[2048,512]{1,0:T(8,128)(2,1)} %edges.7) | copy-start | bytes 6291460
  47.0 10.0 %copy-start.25 = (s32[1,2048]{1,0:T(1,128)S(1)}, s32[1,2048]{1,0:T(1,128)}, u32[]{:S(2)}) copy-start(s32[1,2048]{1,0:T(1,128)} %receivers.11) | copy-start | bytes 24580
  47.0 39.3 %all-to-all-start = ((bf16[128,16,512]{2,1,0:T(8,128)(2,1)}), bf16[128,16,512]{2,1,0:T(8,128)(2,1)}, u32[]{:S(2)}, u32[]{:S(2)}) async-start(bf16[128,16,512]{2,1,0:T(8,128)(2,1)} %bitcast.60), calls=%async_computation | async-start | bytes 4194304 | tf_op jit(solution)/shard_map/all_to_all | solution.py:279
  57.0 1.0 copy-start.16
  58.0 1.0 copy-start.17
  59.1 27.2 %copy-start.26 = (s32[1,2048]{1,0:T(1,128)S(1)}, s32[1,2048]{1,0:T(1,128)}, u32[]{:S(2)}) copy-start(s32[1,2048]{1,0:T(1,128)} %param.21) | copy-start | bytes 24580
  62.6 2.0 %copy-start = (f32[2048,512]{1,0:T(8,128)}, f32[2048,512]{1,0:T(8,128)S(1)}, u32[]{:S(2)}) copy-start(f32[2048,512]{1,0:T(8,128)S(1)} %pre_next.2.pre) | copy-start | bytes 12582916
  86.3 2.2 %copy-start.1 = (f32[2048,512]{1,0:T(8,128)S(1)}, f32[2048,512]{1,0:T(8,128)}, u32[]{:S(2)}) copy-start(f32[2048,512]{1,0:T(8,128)} %copy-done) | copy-start | bytes 12582916
  88.5 1.2 copy-start.7
  89.7 1.0 copy-start.13
  90.8 1.0 copy-start.14
  91.8 1.0 copy-start.15
  92.9 1.0 copy-start.19
  93.9 0.7 copy-start.27
  94.6 0.7 copy-start.28
  109.5 1.3 copy-start.5
  110.8 1.4 copy-start.21
  112.2 0.7 copy-start.23
  112.9 5.9 %copy-start.6 = (bf16[2048,512]{1,0:T(8,128)(2,1)S(1)}, bf16[2048,512]{1,0:T(8,128)(2,1)}, u32[]{:S(2)}) copy-start(bf16[2048,512]{1,0:T(8,128)(2,1)} %copy-done.5) | copy-start | bytes 6291460
  112.9 35.3 %all-to-all-start.1 = ((bf16[128,16,512]{2,1,0:T(8,128)(2,1)}), bf16[128,16,512]{2,1,0:T(8,128)(2,1)}, u32[]{:S(2)}, u32[]{:S(2)}) async-start(bf16[128,16,512]{2,1,0:T(8,128)(2,1)} %bitcast.61), calls=%async_computation.1 | async-start | bytes 4194304 | tf_op jit(solution)/shard_map/all_to_all | solution.py:279
  118.8 1.0 copy-start.11
  119.8 1.0 copy-start.12
  120.9 27.3 %copy-start.24 = (bf16[128,512]{1,0:T(8,128)(2,1)S(1)}, bf16[128,512]{1,0:T(8,128)(2,1)}, u32[]{:S(2)}) copy-start(bf16[128,512]{1,0:T(8,128)(2,1)} %copy-done.23) | copy-start | bytes 393220
  120.9 27.3 %copy-start.29 = (f32[2,512]{1,0:T(2,128)S(1)}, f32[2,512]{1,0:T(2,128)}, u32[]{:S(2)}) copy-start(f32[2,512]{1,0:T(2,128)} %get-tuple-element.45.node_norm) | copy-start | bytes 12292
  120.9 27.3 %copy-start.30 = (f32[2,512]{1,0:T(2,128)S(1)}, f32[2,512]{1,0:T(2,128)}, u32[]{:S(2)}) copy-start(f32[2,512]{1,0:T(2,128)} %get-tuple-element.50.edge_norm) | copy-start | bytes 12292
  124.4 2.0 %copy-start.2 = (f32[2048,512]{1,0:T(8,128)}, f32[2048,512]{1,0:T(8,128)S(1)}, u32[]{:S(2)}) copy-start(f32[2048,512]{1,0:T(8,128)S(1)} %pre_next.3.pre) | copy-start | bytes 12582916
  148.1 2.2 %copy-start.3 = (f32[2048,512]{1,0:T(8,128)S(1)}, f32[2048,512]{1,0:T(8,128)}, u32[]{:S(2)}) copy-start(f32[2048,512]{1,0:T(8,128)} %copy-done.2) | copy-start | bytes 12582916
  150.3 1.0 copy-start.9
  151.4 1.0 copy-start.10

commit v2 on v1

v2 whole, which is shorter than its diff:
```python
import functools

import jax
import jax.numpy as jnp
from jax import lax
from jax.experimental import pallas as pl
from jax.experimental.pallas import tpu as pltpu
from jax.sharding import PartitionSpec as P

HALO = 4
NORM_EPS = 1e-05
F32 = jnp.float32
BF16 = jnp.bfloat16
I32 = jnp.int32
BLOCK = 256
CHUNK = 256
LANES = 128
MIB = 1024 * 1024


def silu(values):
    half = values * 0.5
    return half + half * jnp.tanh(half)


def normalize(values, gains, biases):
    centre = jnp.mean(values, axis=-1, keepdims=True)
    shifted = values - centre
    spread = jnp.mean(shifted * shifted, axis=-1, keepdims=True)
    return shifted * lax.rsqrt(spread + NORM_EPS) * gains + biases


def dot(left, right):
    return jnp.dot(left, right, preferred_element_type=F32)


def project(values, weights):
    return dot(values, weights).astype(BF16)


def hot_columns(indices, nodes):
    places = lax.broadcasted_iota(I32, (nodes, indices.shape[1]), 0)
    return jnp.where(places == indices, 1.0, 0.0)


def hot_rows(indices, nodes):
    return hot_columns(indices, nodes).T.astype(BF16)


def line_of(row, tiles):
    return (row >> 3) * (8 * tiles) + (row & 7)


def cell_row(cell, high, wide):
    across = wide + 2 * HALO
    row = (cell * 241) >> 15
    column = cell - row * across
    band = jnp.where(row < HALO, 1, jnp.where(row < HALO + high, 0, 2))
    inner = row - jnp.where(band == 1, 0, jnp.where(band == 0, HALO, HALO + high))
    cells = high * wide
    tall = (high + 2 * HALO) * HALO
    side = 3 * cells + row * HALO
    west = side + column
    east = side + tall + column - HALO - wide
    centre = band * cells + inner * wide + column - HALO
    return jnp.where(column < HALO, west, jnp.where(column < HALO + wide, centre, east))


def begin(source, target, sem):
    copy = pltpu.make_async_copy(source, target, sem)
    copy.start()
    return copy


def part(ref, i):
    return ref.at[pl.ds(pl.multiple_of(i * BLOCK, BLOCK), BLOCK)]


def pre_kernel(level, shape, edges_h, receivers_h, nodes_h, edge_in_h, *refs):
    refs = list(refs)
    take = lambda count: [refs.pop(0) for _ in range(count)]
    if shape:
        tile_h, send_rows_h, cells_h, senders_h = take(4)
    pre_h = take(1)[0]
    if shape:
        tile_terms_h, picks_h, places_h, lines_h = take(4)
    edges, receivers, nodes, w_edge, w_recv, pre = take(6)
    if shape:
        tile, w_send, send_rows, cells, senders, tile_terms, picks, places, lines = take(9)
    sems, edge_sems, out_sems = take(3)
    node_count = nodes.shape[0]
    blocks = edges.shape[0] // BLOCK

    def edge_copy(i):
        return pltpu.make_async_copy(part(edges_h, i), part(edges, i), edge_sems.at[i])

    def out_copy(i):
        return pltpu.make_async_copy(part(pre, i), part(pre_h, i), out_sems.at[i])

    first = [
        begin(nodes_h, nodes, sems.at[0]),
        begin(edge_in_h.at[level, 2], w_recv, sems.at[1]),
        begin(receivers_h, receivers, sems.at[2]),
        begin(edge_in_h.at[level, 0], w_edge, sems.at[3]),
    ]
    for i in range(blocks):
        edge_copy(i).start()
    if shape:
        second = [
            begin(tile_h, tile, sems.at[4]),
            begin(edge_in_h.at[level, 1], w_send, sems.at[5]),
            begin(send_rows_h, send_rows, sems.at[6]),
            begin(cells_h, cells, sems.at[7]),
            begin(senders_h, senders, sems.at[8]),
        ]
    for copy in first:
        copy.wait()
    terms = project(nodes[...], w_recv[...])

    def step(i, _):
        rows = pl.ds(pl.multiple_of(i * BLOCK, BLOCK), BLOCK)
        edge_copy(i).wait()
        hot = hot_rows(jnp.minimum(receivers[:, rows], node_count - 1), node_count)
        pre[rows, :] = dot(edges[rows, :], w_edge[...]) + dot(hot, terms)
        out_copy(i).start()
        return 0

    lax.fori_loop(0, blocks, step, 0)
    if shape:
        high, wide = shape
        tiles = edges.shape[1] // LANES
        for copy in second:
            copy.wait()
        tile_terms[...] = project(tile[...], w_send[...])
        ends = [begin(tile_terms, tile_terms_h, sems.at[9])]

        def pick(i, _):
            rows = pl.ds(pl.multiple_of(i * BLOCK, BLOCK), BLOCK)
            picks[rows, :] = hot_rows(send_rows[:, rows], node_count)
            return 0

        lax.fori_loop(0, picks.shape[0] // BLOCK, pick, 0)
        ends.append(begin(picks, picks_h, sems.at[10]))
        places[...] = line_of(cell_row(cells[...], high, wide), tiles)
        lines[...] = line_of(senders[...], tiles)
        ends.append(begin(places, places_h, sems.at[11]))
        ends.append(begin(lines, lines_h, sems.at[12]))
    for i in range(blocks):
        out_copy(i).wait()
    if shape:
        for copy in ends:
            copy.wait()


def fill_table(table, start, values):
    tiles = values.shape[1] // LANES
    for group in range(values.shape[0] // 8):
        for tile in range(tiles):
            line = pl.multiple_of(start * tiles + (group * tiles + tile) * 8, 8)
            table[pl.ds(line, 8), :] = values[group * 8:group * 8 + 8, tile * LANES:(tile + 1) * LANES]


def main_kernel(level, pieces, last, keep, *refs):
    refs = list(refs)
    take = lambda count: [refs.pop(0) for _ in range(count)]
    places_h, receivers_h, pre_h, edges_h, nodes_h = take(5)
    edge_in_h, edge_out_h, node_in_h, node_out_h, gain_h, bias_h = take(6)
    sources = take(pieces)
    picks_h = None if last else take(1)[0]
    new_nodes_h = take(1)[0]
    outgoing_h, out_rows_h = (None, None) if last else take(2)
    new_edges_h = take(1)[0] if keep else None
    table, hidden_0, hidden_1, total, places, receivers, pre, edges = take(8)
    nodes, w_out, w_node, w_node_out, gain, bias, new_nodes, local_rows = take(8)
    w_send = take(1)[0] if pieces > 2 else None
    w_next, picks, outgoing, out_rows = (None,) * 4 if last else take(4)
    fresh_edges = take(1)[0] if keep else None
    sems, pre_sems, edge_sems, out_sems = take(4)

    node_count, width = nodes.shape
    blocks = edges.shape[0] // BLOCK
    tiles = width // LANES

    def pre_copy(i):
        return pltpu.make_async_copy(part(pre_h, i), part(pre, i), pre_sems.at[i])

    def edge_copy(i):
        return pltpu.make_async_copy(part(edges_h, i), part(edges, i), edge_sems.at[i])

    def fresh_copy(i):
        return pltpu.make_async_copy(part(fresh_edges, i), part(new_edges_h, i), out_sems.at[i])

    local_copy = begin(sources[0], local_rows, sems.at[0])
    places_copy = begin(places_h, places, sems.at[1])
    if w_send is not None:
        send_copy = begin(edge_in_h.at[level, 1], w_send, sems.at[2])
    pre_copy(0).start()
    second = [
        begin(edge_out_h.at[level], w_out, sems.at[3]),
        begin(receivers_h, receivers, sems.at[4]),
        begin(gain_h, gain, sems.at[5]),
        begin(bias_h, bias, sems.at[6]),
    ]
    edge_copy(0).start()
    for i in range(1, blocks):
        pre_copy(i).start()
        edge_copy(i).start()
    third = [
        begin(nodes_h, nodes, sems.at[7]),
        begin(node_in_h.at[level], w_node, sems.at[8]),
        begin(node_out_h.at[level], w_node_out, sems.at[9]),
    ]
    if not last:
        third.append(begin(edge_in_h.at[level + 1, 1], w_next, sems.at[10]))
        third.append(begin(picks_h, picks, sems.at[11]))

    total[...] = jnp.zeros_like(total)
    start = local_rows.shape[0]
    if w_send is not None:
        send_copy.wait()
    for source in sources[1:]:
        size = source.shape[0]
        for at in range(0, size, min(size, CHUNK)):
            values = source[at:at + min(size, CHUNK), :]
            if w_send is not None:
                values = project(values, w_send[...])
            fill_table(table, start + at, values.astype(F32))
        start += size
    local_copy.wait()
    fill_table(table, 0, local_rows[...].astype(F32))
    places_copy.wait()

    sublane = lax.broadcasted_iota(I32, (8, LANES), 0)
    chosen = [sublane == j for j in range(8)]

    def found(at):
        lines = [places[0, at + j] for j in range(8)]
        result = []
        for tile in range(tiles):
            value = None
            for j in range(8):
                row = jnp.broadcast_to(table[pl.ds(lines[j] + 8 * tile, 1), :], (8, LANES))
                value = row if j == 0 else jnp.where(chosen[j], row, value)
            result.append(value)
        return result

    def gather(i, hidden):
        at = pl.multiple_of(i * BLOCK, BLOCK)
        for group in range(BLOCK // 16):
            halves = []
            for half in range(2):
                offset = group * 16 + half * 8
                rows = found(at + offset)
                lead = pl.ds(pl.multiple_of(at + offset, 8), 8)
                halves.append([
                    silu(pre[lead, t * LANES:(t + 1) * LANES] + rows[t]) for t in range(tiles)
                ])
            for t in range(tiles):
                both = jnp.concatenate([halves[0][t], halves[1][t]], axis=0).astype(BF16)
                hidden[group * 16:group * 16 + 16, t * LANES:(t + 1) * LANES] = both

    def update(i, hidden):
        rows = pl.ds(pl.multiple_of(i * BLOCK, BLOCK), BLOCK)
        output = dot(hidden[...], w_out[...])
        fresh = normalize(output, gain[level, 0:1, :], bias[level, 0:1, :])
        fresh = (edges[rows, :].astype(F32) + fresh).astype(BF16)
        if keep:
            fresh_edges[rows, :] = fresh
        total[...] += dot(hot_columns(receivers[:, rows], node_count).astype(BF16), fresh)

    def both(i, ready, filling):
        pre_copy(i + 1).wait()
        edge_copy(i).wait()
        gather(i + 1, filling)
        update(i, ready)
        if keep:
            fresh_copy(i).start()

    pre_copy(0).wait()
    gather(0, hidden_0)
    for copy in second:
        copy.wait()

    def step(pair, _):
        both(2 * pair, hidden_0, hidden_1)
        both(2 * pair + 1, hidden_1, hidden_0)
        return 0

    lax.fori_loop(0, blocks // 2 - 1, step, 0)
    both(blocks - 2, hidden_0, hidden_1)
    edge_copy(blocks - 1).wait()
    update(blocks - 1, hidden_1)
    if keep:
        fresh_copy(blocks - 1).start()

    for copy in third:
        copy.wait()
    here = nodes[...]
    pre_node = dot(here, w_node[0]) + dot(total[...].astype(BF16), w_node[1])
    output = dot(silu(pre_node).astype(BF16), w_node_out[...])
    updated = here.astype(F32) + normalize(output, gain[level, 1:2, :], bias[level, 1:2, :])
    updated = updated.astype(BF16)
    new_nodes[...] = updated
    ends = [begin(new_nodes, new_nodes_h, sems.at[12])]
    if not last:
        sent = project(updated, w_next[...])
        outgoing[...] = sent
        ends.append(begin(outgoing, outgoing_h, sems.at[13]))
        for i in range(out_rows.shape[0] // BLOCK):
            rows = pl.ds(i * BLOCK, BLOCK)
            out_rows[rows, :] = dot(picks[rows, :], sent).astype(BF16)
            ends.append(begin(out_rows.at[rows], out_rows_h.at[rows], pre_sems.at[i]))
    if keep:
        for i in range(blocks):
            fresh_copy(i).wait()
    for copy in ends:
        copy.wait()


HBM = pl.BlockSpec(memory_space=pltpu.HBM)
VMEM = pl.BlockSpec(memory_space=pltpu.VMEM)


def pre_stage(level, edges, receivers, nodes, edge_in, extra=(), shape=None):
    edge_count, width = edges.shape
    node_count = nodes.shape[0]
    blocks = edge_count // BLOCK
    operands = [edges, receivers, nodes, edge_in, *extra]
    out_shape = [pltpu.HBM((edge_count, width), F32)]
    line = pltpu.VMEM((1, edge_count), I32)
    weight = pltpu.VMEM((width, width), BF16)
    scratch = [
        pltpu.VMEM((edge_count, width), BF16), line, pltpu.VMEM((node_count, width), BF16),
        weight, weight, pltpu.VMEM((edge_count, width), F32),
    ]
    if shape:
        tile, send_rows = extra[:2]
        out_shape += [
            pltpu.HBM(tile.shape, BF16),
            pltpu.HBM((send_rows.shape[1], node_count), BF16),
            pltpu.HBM((1, edge_count), I32),
            pltpu.HBM((1, edge_count), I32),
        ]
        tiled = pltpu.VMEM(tile.shape, BF16)
        scratch += [
            tiled, weight, pltpu.VMEM(send_rows.shape, I32), line, line, tiled,
            pltpu.VMEM((send_rows.shape[1], node_count), BF16), line, line,
        ]
    scratch += [pltpu.SemaphoreType.DMA((n,)) for n in (13, blocks, blocks)]
    return pl.pallas_call(
        functools.partial(pre_kernel, level, shape),
        out_shape=out_shape,
        in_specs=[HBM] * len(operands),
        out_specs=[HBM] * len(out_shape),
        scratch_shapes=scratch,
        name="pre_first" if shape else "pre_next",
        cost_estimate=pl.CostEstimate(
            flops=2 * edge_count * width * (width + node_count),
            bytes_accessed=edge_count * width * 6,
            transcendentals=0,
        ),
        compiler_params=pltpu.CompilerParams(vmem_limit_bytes=20 * MIB),
    )(*[pltpu.with_memory_space_constraint(operand, pltpu.HBM) for operand in operands])


def main_stage(level, places, receivers, pre, edges, nodes, weights, tables, picks, last, keep):
    edge_count, width = edges.shape
    node_count = nodes.shape[0]
    operands = [places, receivers, pre, edges, nodes, *weights, *tables]
    in_specs = [HBM] * 12 + [VMEM] * (len(tables) - 1)
    out_shape = [pltpu.HBM((node_count, width), BF16)]
    blocks = edge_count // BLOCK
    table_rows = sum(piece.shape[0] for piece in tables)
    norm = pltpu.VMEM(weights[4].shape, F32)
    small = pltpu.VMEM((node_count, width), BF16)
    weight = pltpu.VMEM((width, width), BF16)
    scratch = [
        pltpu.VMEM((table_rows * (width // LANES), LANES), F32),
        pltpu.VMEM((BLOCK, width), BF16),
        pltpu.VMEM((BLOCK, width), BF16),
        pltpu.VMEM((node_count, width), F32),
        pltpu.SMEM((1, edge_count), I32),
        pltpu.VMEM((1, edge_count), I32),
        pltpu.VMEM((edge_count, width), F32),
        pltpu.VMEM((edge_count, width), BF16),
        small, weight, pltpu.VMEM((2, width, width), BF16), weight, norm, norm, small,
        pltpu.VMEM(tables[0].shape, BF16),
    ]
    if len(tables) > 2:
        scratch.append(weight)
    if not last:
        operands.append(picks)
        in_specs.append(HBM)
        rows = picks.shape[0]
        out_shape.append(pltpu.HBM((node_count, width), BF16))
        out_shape.append(pltpu.HBM((rows, width), BF16))
        scratch += [weight, pltpu.VMEM(picks.shape, BF16), small, pltpu.VMEM((rows, width), BF16)]
    if keep:
        out_shape.append(pltpu.HBM((edge_count, width), BF16))
        scratch.append(pltpu.VMEM((edge_count, width), BF16))
    scratch += [pltpu.SemaphoreType.DMA((n,)) for n in (14, blocks, blocks, blocks)]
    operands = [
        pltpu.with_memory_space_constraint(operand, pltpu.HBM) if spec is HBM else operand
        for operand, spec in zip(operands, in_specs)
    ]
    return pl.pallas_call(
        functools.partial(main_kernel, level, len(tables), last, keep),
        out_shape=out_shape,
        in_specs=in_specs,
        out_specs=[HBM] * len(out_shape),
        scratch_shapes=scratch,
        name="encode" if level == 0 else "layer",
        cost_estimate=pl.CostEstimate(
            flops=2 * edge_count * width * (width + node_count),
            bytes_accessed=edge_count * width * 10,
            transcendentals=edge_count * width,
        ),
        compiler_params=pltpu.CompilerParams(vmem_limit_bytes=32 * MIB),
    )(*operands)


def shift(array, axis, step, wrap):
    size = lax.axis_size(axis)
    pairs = [(i, (i + step) % size) for i in range(size) if wrap or 0 <= i + step < size]
    return lax.ppermute(array, axis, pairs)


def local(
    grid_latent,
    mesh_latent,
    g2m_edges,
    g2m_senders,
    g2m_receivers,
    mm_edges,
    mm_senders,
    mm_receivers,
    send_rows,
    edge_in,
    edge_out,
    node_in,
    node_out,
    norm_gain,
    norm_bias,
):
    high, wide, features = grid_latent.shape
    flat_tile = grid_latent.reshape(high * wide, features)
    weights = [edge_in, edge_out, node_in, node_out, norm_gain, norm_bias]

    north = shift(grid_latent, "lat", 1, False)
    south = shift(grid_latent, "lat", -1, False)
    pre, tile_terms, picks, places, lines = pre_stage(
        0, g2m_edges, g2m_receivers, mesh_latent, edge_in,
        (flat_tile, send_rows, g2m_senders, mm_senders), (high, wide),
    )
    north, south, tile_terms = lax.optimization_barrier((north, south, tile_terms))

    def column(first):
        pieces = [piece[:, first:first + HALO] for piece in (north, grid_latent, south)]
        return jnp.concatenate(pieces, axis=0).reshape(-1, features)

    west = shift(column(wide - HALO), "lon", 1, True)
    east = shift(column(0), "lon", -1, True)
    tables = [tile_terms, north.reshape(-1, features), south.reshape(-1, features), west, east]
    nodes, outgoing, out_rows = main_stage(
        0, places, g2m_receivers, pre, g2m_edges, mesh_latent, weights, tables, picks, False, False
    )
    edges = mm_edges
    levels = edge_in.shape[0]
    devices = lax.axis_size("lat") * lax.axis_size("lon")
    for level in range(1, levels):
        blocks = out_rows.reshape(devices, -1, features)
        arrived = lax.all_to_all(blocks, ("lat", "lon"), split_axis=0, concat_axis=0, tiled=True)
        arrived = arrived.reshape(-1, features)
        (pre,) = pre_stage(level, edges, mm_receivers, nodes, edge_in)
        last = level == levels - 1
        results = main_stage(
            level, lines, mm_receivers, pre, edges, nodes, weights, [outgoing, arrived], picks,
            last, not last,
        )
        if last:
            (nodes,) = results
        else:
            nodes, outgoing, out_rows, edges = results
    return nodes


def solution(mesh):
    in_specs = (
        P("lat", "lon", None),
        P(("lat", "lon"), None),
        P(("lat", "lon"), None),
        P(("lat", "lon"), None),
        P(("lat", "lon"), None),
        P(("lat", "lon"), None),
        P(("lat", "lon"), None),
        P(("lat", "lon"), None),
        P(("lat", "lon"), None),
        P(),
        P(),
        P(),
        P(),
        P(),
        P(),
    )
    out_specs = P(("lat", "lon"), None)
    return jax.shard_map(local, mesh=mesh, in_specs=in_specs, out_specs=out_specs, check_vma=False)
```

time: 167 us -> 130 us (0.78)
  local copies, waits for them, and re-layouts: 35.5 us -> 0.86 us
  waiting for transfers between devices: 43.7 us -> 48.6 us
  starting transfers between devices: 31.6 us -> 27 us
  other arithmetic: 2.15 us -> 0.08 us
    unnamed x78 -> x0, local copies, waits for them, and re-layouts: 28.3 us -> none
    squeeze x3 -> x0, local copies, waits for them, and re-layouts: 6.38 us -> none  [the longest x1 3.35 us: local(): node_in[level]]
    ppermute x6 -> x4, starting transfers between devices: 15.7 us -> 9.8 us  [shift(): return lax.ppermute(array, axis, pairs)]
    all_to_all x2, waiting for transfers between devices: 43.5 us -> 46.6 us  [local(): lax.all_to_all(blocks, ('lat', 'lon'), split_axis=0, concat_axis=0, tiled...]
    ppermute x6 -> x4, waiting for transfers between devices: 0.23 us -> 2 us  [shift(): return lax.ppermute(array, axis, pairs)]
  transfers between devices with their start and end apart: 8 -> 6, of which waited for: 3 -> 3; matrix products, arithmetic and copies ran while one was open for 6% -> 1% of each run, Pallas kernels for 7% -> 16%
where the time goes in v2:
time: 130 us
  Pallas kernels  53.2 us (41%)
  waiting for transfers between devices  48.6 us (37%)
  starting transfers between devices  27 us (21%)
    all_to_all x2, waiting for transfers between devices, local(): lax.all_to_all(blocks, ('lat', 'lon'), split_axis=0, concat_axis=0, tiled...  46.6 us
    pallas_call x3, Pallas kernels, main_stage(): pl.pallas_call(functools.partial(main_kernel, level, len(tables), last, k...  33 us
    pallas_call x3, Pallas kernels, pre_stage(): pl.pallas_call(functools.partial(pre_kernel, level, shape), out_shape=out...  20.2 us
    all_to_all x2, starting transfers between devices, local(): lax.all_to_all(blocks, ('lat', 'lon'), split_axis=0, concat_axis=0, tiled...  17.2 us
    ppermute x4, starting transfers between devices, shift(): return lax.ppermute(array, axis, pairs)  9.8 us
  transfers between devices with their start and end apart: 6, of which 3 were waited for; matrix products, arithmetic and copies ran while one was open for 1% of the time, Pallas kernels for 16%

profile of v2, /device:TPU:0, one launch (start us, length us, event | category | flops | bytes accessed | tf_op | source)
XLA Modules:
  0.0 129.9 jit_solution(3908982458826068367)
XLA Ops:
  0.0 1.3 %collective-permute-start = (bf16[4,128,512]{2,1,0:T(8,128)(2,1)}, bf16[4,128,512]{2,1,0:T(8,128)(2,1)S(1)}, u32[]{:S(2)}, u32[]{:S(2)}) collective-permute-start(bf16[4,128,512]{2,1,0:T(8,128)(2,1)} %param.15), channel_id=1, source_target_pairs={{0,16},{16,32},{32,48},{48,64},{64,80},{80,96},{96,112},{1,17},{17... | collective-permute-start | bytes 1572872 | tf_op jit(solution)/shard_map/ppermute | solution.py:425
  1.3 1.3 collective-permute-start.1
  2.6 7.4 %pre_first.1 = (f32[2048,512]{1,0:T(8,128)}, bf16[512,512]{1,0:T(8,128)(2,1)}, bf16[2048,128]{1,0:T(8,128)(2,1)}, s32[1,2048]{1,0:T(1,128)}, s32[1,2048]{1,0:T(1,128)}) custom-call(bf16[2048,512]{1,0:T(8,128)(2,1)} %refs_3_.4, s32[1,2048]{1,0:T(1,128)} %refs_1_.5, bf16[128,512]{1,0:T(8,128)(2,1)} %refs_4_.1, bf16[3,3,512,512]{3,2,1,0:T(8,128)(2,1)} %refs_5_.5, ...), custom_call_target="tpu_custom_call" | custom-call | flops 1342177280 | bytes 6291456 | tf_op jit(solution)/shard_map/pre_first/pallas_call | solution.py:350
  10.0 0.8 fusion.1
  10.8 0.0 collective-permute-done
  10.8 0.0 collective-permute-done.1
  11.0 2.2 %collective-permute-start.2 = (bf16[48,512]{1,0:T(8,128)(2,1)S(1)}, bf16[48,512]{1,0:T(8,128)(2,1)S(1)}, u32[]{:S(2)}, u32[]{:S(2)}) collective-permute-start(bf16[48,512]{1,0:T(8,128)(2,1)S(1)} %reshape.30), channel_id=1, source_target_pairs={{0,1},{1,2},{2,3},{3,4},{4,5},{5,6},{6,7},{7,8},{8,9},{9,10},{10,1... | collective-permute-start | bytes 147464 | tf_op jit(solution)/shard_map/ppermute | solution.py:425
  13.2 5.0 %collective-permute-start.3 = (bf16[48,512]{1,0:T(8,128)(2,1)S(1)}, bf16[48,512]{1,0:T(8,128)(2,1)S(1)}, u32[]{:S(2)}, u32[]{:S(2)}) collective-permute-start(bf16[48,512]{1,0:T(8,128)(2,1)S(1)} %reshape.31), channel_id=1, source_target_pairs={{0,15},{1,0},{2,1},{3,2},{4,3},{5,4},{6,5},{7,6},{8,7},{9,8},{10,9... | collective-permute-start | bytes 147464 | tf_op jit(solution)/shard_map/ppermute | solution.py:425
  18.2 2.0 %collective-permute-done.2.refs_14_ = bf16[48,512]{1,0:T(8,128)(2,1)S(1)} collective-permute-done((bf16[48,512]{1,0:T(8,128)(2,1)S(1)}, bf16[48,512]{1,0:T(8,128)(2,1)S(1)}, u32[]{:S(2)}, u32[]{:S(2)}) %collective-permute-start.2) | collective-permute-done | bytes 49184 | tf_op jit(solution)/shard_map/ppermute | solution.py:425
  20.2 0.0 collective-permute-done.3.refs_15_
  20.2 11.8 %encode.1 = (bf16[128,512]{1,0:T(8,128)(2,1)}, bf16[128,512]{1,0:T(8,128)(2,1)}, bf16[2048,512]{1,0:T(8,128)(2,1)}) custom-call(s32[1,2048]{1,0:T(1,128)} %get-tuple-element.21.refs_0_, s32[1,2048]{1,0:T(1,128)} %refs_1_.5, f32[2048,512]{1,0:T(8,128)} %get-tuple-element.22.refs_2_, bf16[2048,512]{1,0:T(8,128)(2,1)} %refs_3_.4, bf16[128,512]{1,0:T(8,128)(2,1)} %refs_4_.1, ...), custom_call_target="tpu_custom_call" | custom-call | flops 1342177280 | bytes 10485760 | tf_op jit(solution)/shard_map/encode/pallas_call | solution.py:406
  32.0 12.5 %all-to-all-start = ((bf16[128,16,512]{2,1,0:T(8,128)(2,1)}), bf16[128,16,512]{2,1,0:T(8,128)(2,1)S(1)}, u32[]{:S(2)}, u32[]{:S(2)}) async-start(bf16[128,16,512]{2,1,0:T(8,128)(2,1)} %bitcast.11), calls=%async_computation | async-start | bytes 4194304 | tf_op jit(solution)/shard_map/all_to_all | solution.py:472
  44.5 6.4 %pre_next.2.refs_2_ = f32[2048,512]{1,0:T(8,128)} custom-call(bf16[2048,512]{1,0:T(8,128)(2,1)} %refs_3_.5, s32[1,2048]{1,0:T(1,128)} %refs_1_.7, bf16[128,512]{1,0:T(8,128)(2,1)} %get-tuple-element.28.nodes_h.refs_4_, bf16[3,3,512,512]{3,2,1,0:T(8,128)(2,1)} %refs_5_.5), custom_call_target="tpu_custom_call" | custom-call | flops 1342177280 | bytes 6291456 | tf_op jit(solution)/shard_map/pre_next/pallas_call | solution.py:350
  50.9 23.2 %all-to-all-done = bf16[128,16,512]{2,1,0:T(8,128)(2,1)S(1)} async-done(((bf16[128,16,512]{2,1,0:T(8,128)(2,1)}), bf16[128,16,512]{2,1,0:T(8,128)(2,1)S(1)}, u32[]{:S(2)}, u32[]{:S(2)}) %all-to-all-start) | async-done | bytes 2097184 | tf_op jit(solution)/shard_map/all_to_all | solution.py:472
  74.1 11.1 %layer.2 = (bf16[128,512]{1,0:T(8,128)(2,1)}, bf16[128,512]{1,0:T(8,128)(2,1)}, bf16[2048,512]{1,0:T(8,128)(2,1)}, bf16[2048,512]{1,0:T(8,128)(2,1)}) custom-call(s32[1,2048]{1,0:T(1,128)} %get-tuple-element.20.refs_0_, s32[1,2048]{1,0:T(1,128)} %refs_1_.7, f32[2048,512]{1,0:T(8,128)} %pre_next.2.refs_2_, bf16[2048,512]{1,0:T(8,128)(2,1)} %refs_3_.5, ...), custom_call_target="tpu_custom_call" | custom-call | flops 1342177280 | bytes 10485760 | tf_op jit(solution)/shard_map/layer/pallas_call | solution.py:406
  85.2 4.7 %all-to-all-start.1 = ((bf16[128,16,512]{2,1,0:T(8,128)(2,1)}), bf16[128,16,512]{2,1,0:T(8,128)(2,1)S(1)}, u32[]{:S(2)}, u32[]{:S(2)}) async-start(bf16[128,16,512]{2,1,0:T(8,128)(2,1)} %bitcast.12), calls=%async_computation.1 | async-start | bytes 4194304 | tf_op jit(solution)/shard_map/all_to_all | solution.py:472
  89.9 6.4 %pre_next.3.refs_2_ = f32[2048,512]{1,0:T(8,128)} custom-call(bf16[2048,512]{1,0:T(8,128)(2,1)} %get-tuple-element.31.edges_h.refs_3_, s32[1,2048]{1,0:T(1,128)} %refs_1_.7, bf16[128,512]{1,0:T(8,128)(2,1)} %get-tuple-element.32.nodes_h.refs_4_, bf16[3,3,512,512]{3,2,1,0:T(8,128)(2,1)} %refs_5_.5), custom_call_target="tpu_custom_call" | custom-call | flops 1342177280 | bytes 6291456 | tf_op jit(solution)/shard_map/pre_next/pallas_call | solution.py:350
  96.3 23.4 %all-to-all-done.1 = bf16[128,16,512]{2,1,0:T(8,128)(2,1)S(1)} async-done(((bf16[128,16,512]{2,1,0:T(8,128)(2,1)}), bf16[128,16,512]{2,1,0:T(8,128)(2,1)S(1)}, u32[]{:S(2)}, u32[]{:S(2)}) %all-to-all-start.1) | async-done | bytes 2097184 | tf_op jit(solution)/shard_map/all_to_all | solution.py:472
  119.6 10.1 %layer.3 = bf16[128,512]{1,0:T(8,128)(2,1)} custom-call(s32[1,2048]{1,0:T(1,128)} %get-tuple-element.20.refs_0_, s32[1,2048]{1,0:T(1,128)} %refs_1_.7, f32[2048,512]{1,0:T(8,128)} %pre_next.3.refs_2_, bf16[2048,512]{1,0:T(8,128)(2,1)} %get-tuple-element.31.edges_h.refs_3_, bf16[128,512]{1,0:T(8,128)(2,1)} %get-tuple-element.32.nodes_h.refs_4_, ...), custom_call_target="tpu_custom_call" | custom-call | flops 1342177280 | bytes 10485760 | tf_op jit(solution)/shard_map/layer/pallas_call | solution.py:406
  (5 shorter events, 0.1 us)
Async XLA Ops:
  0.0 10.8 %collective-permute-start = (bf16[4,128,512]{2,1,0:T(8,128)(2,1)}, bf16[4,128,512]{2,1,0:T(8,128)(2,1)S(1)}, u32[]{:S(2)}, u32[]{:S(2)}) collective-permute-start(bf16[4,128,512]{2,1,0:T(8,128)(2,1)} %param.15), channel_id=1, source_target_pairs={{0,16},{16,32},{32,48},{48,64},{64,80},{80,96},{96,112},{1,17},{17... | collective-permute-start | bytes 1572872 | tf_op jit(solution)/shard_map/ppermute | solution.py:425
  1.3 9.5 %collective-permute-start.1 = (bf16[4,128,512]{2,1,0:T(8,128)(2,1)}, bf16[4,128,512]{2,1,0:T(8,128)(2,1)S(1)}, u32[]{:S(2)}, u32[]{:S(2)}) collective-permute-start(bf16[4,128,512]{2,1,0:T(8,128)(2,1)} %param.15), channel_id=1, source_target_pairs={{16,0},{32,16},{48,32},{64,48},{80,64},{96,80},{112,96},{17,1},{33... | collective-permute-start | bytes 1572872 | tf_op jit(solution)/shard_map/ppermute | solution.py:425
  11.0 9.2 %collective-permute-start.2 = (bf16[48,512]{1,0:T(8,128)(2,1)S(1)}, bf16[48,512]{1,0:T(8,128)(2,1)S(1)}, u32[]{:S(2)}, u32[]{:S(2)}) collective-permute-start(bf16[48,512]{1,0:T(8,128)(2,1)S(1)} %reshape.30), channel_id=1, source_target_pairs={{0,1},{1,2},{2,3},{3,4},{4,5},{5,6},{6,7},{7,8},{8,9},{9,10},{10,1... | collective-permute-start | bytes 147464 | tf_op jit(solution)/shard_map/ppermute | solution.py:425
  13.2 7.0 %collective-permute-start.3 = (bf16[48,512]{1,0:T(8,128)(2,1)S(1)}, bf16[48,512]{1,0:T(8,128)(2,1)S(1)}, u32[]{:S(2)}, u32[]{:S(2)}) collective-permute-start(bf16[48,512]{1,0:T(8,128)(2,1)S(1)} %reshape.31), channel_id=1, source_target_pairs={{0,15},{1,0},{2,1},{3,2},{4,3},{5,4},{6,5},{7,6},{8,7},{9,8},{10,9... | collective-permute-start | bytes 147464 | tf_op jit(solution)/shard_map/ppermute | solution.py:425
  32.0 42.1 %all-to-all-start = ((bf16[128,16,512]{2,1,0:T(8,128)(2,1)}), bf16[128,16,512]{2,1,0:T(8,128)(2,1)S(1)}, u32[]{:S(2)}, u32[]{:S(2)}) async-start(bf16[128,16,512]{2,1,0:T(8,128)(2,1)} %bitcast.11), calls=%async_computation | async-start | bytes 4194304 | tf_op jit(solution)/shard_map/all_to_all | solution.py:472
  85.2 34.4 %all-to-all-start.1 = ((bf16[128,16,512]{2,1,0:T(8,128)(2,1)}), bf16[128,16,512]{2,1,0:T(8,128)(2,1)S(1)}, u32[]{:S(2)}, u32[]{:S(2)}) async-start(bf16[128,16,512]{2,1,0:T(8,128)(2,1)} %bitcast.12), calls=%async_computation.1 | async-start | bytes 4194304 | tf_op jit(solution)/shard_map/all_to_all | solution.py:472

commit v3 on v2

v3 whole, which is shorter than its diff:
```python
import functools

import jax
import jax.numpy as jnp
from jax import lax
from jax.experimental import pallas as pl
from jax.experimental.pallas import tpu as pltpu
from jax.sharding import PartitionSpec as P

HALO = 4
NORM_EPS = 1e-05
F32 = jnp.float32
BF16 = jnp.bfloat16
I32 = jnp.int32
BLOCK = 256
CHUNK = 256
GROUP = 16
PRE_BLOCK = 512
LANES = 128
MIB = 1024 * 1024


def silu_of_half(half):
    return half + half * jnp.tanh(half)


def normalize(values, gains, biases):
    centre = jnp.mean(values, axis=-1, keepdims=True)
    shifted = values - centre
    spread = jnp.mean(shifted * shifted, axis=-1, keepdims=True)
    return shifted * lax.rsqrt(spread + NORM_EPS) * gains + biases


def dot(left, right):
    return jnp.dot(left, right, preferred_element_type=F32)


def project(values, weights):
    return dot(values, weights).astype(BF16)


def hot_columns(indices, nodes):
    places = lax.broadcasted_iota(I32, (nodes, indices.shape[1]), 0)
    return jnp.where(places == indices, 1.0, 0.0)


def hot_rows(indices, nodes):
    return hot_columns(indices, nodes).T.astype(BF16)


def cell_row(cell, high, wide):
    across = wide + 2 * HALO
    row = (cell * 241) >> 15
    column = cell - row * across
    band = jnp.where(row < HALO, 1, jnp.where(row < HALO + high, 0, 2))
    inner = row - jnp.where(band == 1, 0, jnp.where(band == 0, HALO, HALO + high))
    cells = high * wide
    tall = (high + 2 * HALO) * HALO
    side = 3 * cells + row * HALO
    west = side + column
    east = side + tall + column - HALO - wide
    centre = band * cells + inner * wide + column - HALO
    return jnp.where(column < HALO, west, jnp.where(column < HALO + wide, centre, east))


def begin(source, target, sem):
    copy = pltpu.make_async_copy(source, target, sem)
    copy.start()
    return copy


def part(ref, i, size=BLOCK):
    return ref.at[pl.ds(pl.multiple_of(i * size, size), size)]


def pre_kernel(level, shape, edges_h, receivers_h, nodes_h, edge_in_h, *refs):
    refs = list(refs)
    take = lambda count: [refs.pop(0) for _ in range(count)]
    if shape:
        tile_h, cells_h, senders_h = take(3)
    pre_h = take(1)[0]
    if shape:
        tile_terms_h, places_h, lines_h = take(3)
    edges, receivers, nodes, w_edge, w_recv, pre = take(6)
    if shape:
        tile, w_send, cells, senders, tile_terms, places, lines = take(7)
    sems, edge_sems, out_sems = take(3)
    node_count = nodes.shape[0]
    blocks = edges.shape[0] // PRE_BLOCK

    def edge_copy(i):
        return pltpu.make_async_copy(part(edges_h, i, PRE_BLOCK), part(edges, i, PRE_BLOCK), edge_sems.at[i])

    def out_copy(i):
        return pltpu.make_async_copy(part(pre, i, PRE_BLOCK), part(pre_h, i, PRE_BLOCK), out_sems.at[i])

    first = [
        begin(nodes_h, nodes, sems.at[0]),
        begin(edge_in_h.at[level, 2], w_recv, sems.at[1]),
        begin(receivers_h, receivers, sems.at[2]),
        begin(edge_in_h.at[level, 0], w_edge, sems.at[3]),
    ]
    edge_copy(0).start()
    if shape:
        second = [
            begin(tile_h, tile, sems.at[4]),
            begin(edge_in_h.at[level, 1], w_send, sems.at[5]),
            begin(cells_h, cells, sems.at[6]),
            begin(senders_h, senders, sems.at[7]),
        ]
    for i in range(1, blocks):
        edge_copy(i).start()
    for copy in first:
        copy.wait()
    terms = project(nodes[...], w_recv[...])

    def step(i, _):
        rows = pl.ds(pl.multiple_of(i * PRE_BLOCK, PRE_BLOCK), PRE_BLOCK)
        edge_copy(i).wait()
        hot = hot_rows(jnp.minimum(receivers[:, rows], node_count - 1), node_count)
        pre[rows, :] = 0.5 * (dot(edges[rows, :], w_edge[...]) + dot(hot, terms))
        out_copy(i).start()
        return 0

    lax.fori_loop(0, blocks, step, 0)
    if shape:
        high, wide = shape
        tiles = edges.shape[1] // LANES
        for copy in second:
            copy.wait()
        tile_terms[...] = project(tile[...], w_send[...])
        ends = [begin(tile_terms, tile_terms_h, sems.at[8])]
        places[...] = cell_row(cells[...], high, wide) * tiles
        lines[...] = senders[...] * tiles
        ends.append(begin(places, places_h, sems.at[9]))
        ends.append(begin(lines, lines_h, sems.at[10]))
    for i in range(blocks):
        out_copy(i).wait()
    if shape:
        for copy in ends:
            copy.wait()


def halo_kernel(node_count, north, south, send_rows_h, edge_in_h, terms, picks_h, send_rows, w_send, picks, sems):
    copies = [
        begin(edge_in_h.at[0, 1], w_send, sems.at[0]),
        begin(send_rows_h, send_rows, sems.at[1]),
    ]
    for copy in copies:
        copy.wait()
    size = north.shape[0]
    terms[0:size, :] = project(north[...], w_send[...])
    terms[size:2 * size, :] = project(south[...], w_send[...])

    def pick(i, _):
        rows = pl.ds(pl.multiple_of(i * BLOCK, BLOCK), BLOCK)
        picks[rows, :] = hot_rows(send_rows[:, rows], node_count)
        return 0

    lax.fori_loop(0, picks.shape[0] // BLOCK, pick, 0)
    begin(picks, picks_h, sems.at[2]).wait()


def fill_table(table, start, values):
    tiles = values.shape[1] // LANES
    for group in range(values.shape[0] // 8):
        for tile in range(tiles):
            lines = pl.ds((start + group * 8) * tiles + tile, 8, stride=tiles)
            table[lines, :] = values[group * 8:group * 8 + 8, tile * LANES:(tile + 1) * LANES]


def main_kernel(level, raw, last, keep, *refs):
    refs = list(refs)
    take = lambda count: [refs.pop(0) for _ in range(count)]
    places_h, receivers_h, pre_h, edges_h, nodes_h = take(5)
    edge_in_h, edge_out_h, node_in_h, node_out_h, gain_h, bias_h = take(6)
    local_h, rows_in = take(2)
    raw_rows = take(raw)
    picks_h = None if last else take(1)[0]
    new_nodes_h = take(1)[0]
    outgoing_h, out_rows_h = (None, None) if last else take(2)
    new_edges_h = take(1)[0] if keep else None
    table, stage_0, stage_1, hidden_0, hidden_1, output_0, output_1 = take(7)
    total, places, receivers, pre, edges = take(5)
    nodes, w_out, w_node, w_node_out, gain, bias, new_nodes, local_rows, fresh_edges = take(9)
    w_send = take(1)[0] if raw else None
    w_next, picks, outgoing, out_rows = (None,) * 4 if last else take(4)
    sems, pre_sems, edge_sems, out_sems = take(4)

    node_count, width = nodes.shape
    blocks = edges.shape[0] // BLOCK
    tiles = width // LANES
    stages = [stage_0, stage_1]
    hidden = [hidden_0, hidden_1]
    outputs = [output_0, output_1]

    def pre_copy(i):
        return pltpu.make_async_copy(part(pre_h, i), part(pre, i), pre_sems.at[i])

    def edge_copy(i):
        return pltpu.make_async_copy(part(edges_h, i), part(edges, i), edge_sems.at[i])

    def fresh_copy(i):
        return pltpu.make_async_copy(part(fresh_edges, i), part(new_edges_h, i), out_sems.at[i])

    places_copy = begin(places_h, places, sems.at[1])
    local_copy = begin(local_h, local_rows, sems.at[0])
    if raw:
        send_copy = begin(edge_in_h.at[level, 1], w_send, sems.at[2])
    pre_copy(0).start()
    second = [
        begin(edge_out_h.at[level], w_out, sems.at[3]),
        begin(receivers_h, receivers, sems.at[4]),
        begin(gain_h, gain, sems.at[5]),
        begin(bias_h, bias, sems.at[6]),
    ]
    pre_copy(1).start()
    for i in range(blocks):
        edge_copy(i).start()
        if i + 2 < blocks:
            pre_copy(i + 2).start()
    third = [
        begin(nodes_h, nodes, sems.at[7]),
        begin(node_in_h.at[level], w_node, sems.at[8]),
        begin(node_out_h.at[level], w_node_out, sems.at[9]),
    ]
    if not last:
        third.append(begin(edge_in_h.at[level + 1, 1], w_next, sems.at[10]))
        third.append(begin(picks_h, picks, sems.at[11]))

    total[...] = jnp.zeros_like(total)
    start = local_rows.shape[0]
    for at in range(0, rows_in.shape[0], CHUNK):
        fill_table(table, start + at, rows_in[at:at + CHUNK, :].astype(F32) * 0.5)
    start += rows_in.shape[0]
    local_copy.wait()
    fill_table(table, 0, local_rows[...].astype(F32) * 0.5)
    if raw:
        send_copy.wait()
    for source in raw_rows:
        fill_table(table, start, project(source[...], w_send[...]).astype(F32) * 0.5)
        start += source.shape[0]
    places_copy.wait()

    def found(at):
        stage = stages[at // BLOCK % 2]
        base = at % BLOCK * tiles
        for j in range(8):
            stage[base + j * tiles:base + (j + 1) * tiles, :] = table[pl.ds(places[0, at + j], tiles), :]
        return [stage[pl.ds(base + tile, 8, stride=tiles), :] for tile in range(tiles)]

    def gather(i, group):
        halves = []
        for at in range(i * BLOCK + group * GROUP, i * BLOCK + (group + 1) * GROUP, 8):
            rows = found(at)
            halves.append([
                silu_of_half(pre[at:at + 8, t * LANES:(t + 1) * LANES] + rows[t]) for t in range(tiles)
            ])
        for t in range(tiles):
            both = jnp.concatenate([half[t] for half in halves], axis=0).astype(BF16)
            hidden[i % 2][group * GROUP:(group + 1) * GROUP, t * LANES:(t + 1) * LANES] = both

    def settle(i, group):
        rows = slice(i * BLOCK + group * GROUP, i * BLOCK + (group + 1) * GROUP)
        output = outputs[i % 2][group * GROUP:(group + 1) * GROUP, :]
        fresh = normalize(output, gain[level, 0:1, :], bias[level, 0:1, :])
        fresh_edges[rows, :] = (edges[rows, :].astype(F32) + fresh).astype(BF16)

    for turn in range(-2, blocks + 1):
        gathering = turn + 2 if turn + 2 < blocks else None
        multiplying = turn + 1 if 0 <= turn + 1 < blocks else None
        settling = turn if 0 <= turn < blocks else None
        adding = turn - 1 if turn >= 1 else None
        if gathering is not None:
            pre_copy(gathering).wait()
        if settling is not None:
            edge_copy(settling).wait()
        if turn == -1:
            for copy in second:
                copy.wait()
        if keep and adding is not None:
            fresh_copy(adding).start()
        if multiplying is not None:
            outputs[multiplying % 2][...] = dot(hidden[multiplying % 2][...], w_out[...])
        if adding is not None:
            rows = slice(adding * BLOCK, (adding + 1) * BLOCK)
            hot = hot_columns(receivers[:, rows], node_count).astype(BF16)
            total[...] += dot(hot, fresh_edges[rows, :])
        for group in range(BLOCK // GROUP):
            if gathering is not None:
                gather(gathering, group)
            if settling is not None:
                settle(settling, group)

    for copy in third:
        copy.wait()
    here = nodes[...]
    pre_node = dot(here, w_node[0]) + dot(total[...].astype(BF16), w_node[1])
    output = dot(silu_of_half(pre_node * 0.5).astype(BF16), w_node_out[...])
    updated = here.astype(F32) + normalize(output, gain[level, 1:2, :], bias[level, 1:2, :])
    updated = updated.astype(BF16)
    new_nodes[...] = updated
    ends = [begin(new_nodes, new_nodes_h, sems.at[12])]
    if not last:
        sent = project(updated, w_next[...])
        outgoing[...] = sent
        ends.append(begin(outgoing, outgoing_h, sems.at[13]))
        for i in range(out_rows.shape[0] // BLOCK):
            rows = pl.ds(i * BLOCK, BLOCK)
            out_rows[rows, :] = dot(picks[rows, :], sent).astype(BF16)
            ends.append(begin(out_rows.at[rows], out_rows_h.at[rows], pre_sems.at[i]))
    if keep:
        for i in range(blocks):
            fresh_copy(i).wait()
    for copy in ends:
        copy.wait()


HBM = pl.BlockSpec(memory_space=pltpu.HBM)
VMEM = pl.BlockSpec(memory_space=pltpu.VMEM)


def pinned(operands, specs):
    pin = pltpu.with_memory_space_constraint
    return [pin(operand, pltpu.HBM) if spec is HBM else operand for operand, spec in zip(operands, specs)]


def pre_stage(level, edges, receivers, nodes, edge_in, extra=(), shape=None):
    edge_count, width = edges.shape
    node_count = nodes.shape[0]
    blocks = edge_count // PRE_BLOCK
    operands = [edges, receivers, nodes, edge_in, *extra]
    out_shape = [pltpu.HBM((edge_count, width), F32)]
    line = pltpu.VMEM((1, edge_count), I32)
    weight = pltpu.VMEM((width, width), BF16)
    scratch = [
        pltpu.VMEM((edge_count, width), BF16), line, pltpu.VMEM((node_count, width), BF16),
        weight, weight, pltpu.VMEM((edge_count, width), F32),
    ]
    if shape:
        tile = extra[0]
        out_shape += [
            pltpu.HBM(tile.shape, BF16), pltpu.HBM((1, edge_count), I32), pltpu.HBM((1, edge_count), I32),
        ]
        tiled = pltpu.VMEM(tile.shape, BF16)
        scratch += [tiled, weight, line, line, tiled, line, line]
    scratch += [pltpu.SemaphoreType.DMA((n,)) for n in (11, blocks, blocks)]
    in_specs = [HBM] * len(operands)
    return pl.pallas_call(
        functools.partial(pre_kernel, level, shape),
        out_shape=out_shape,
        in_specs=in_specs,
        out_specs=[HBM] * len(out_shape),
        scratch_shapes=scratch,
        name="pre_first" if shape else "pre_next",
        cost_estimate=pl.CostEstimate(
            flops=2 * edge_count * width * (width + node_count),
            bytes_accessed=edge_count * width * 6,
            transcendentals=0,
        ),
        compiler_params=pltpu.CompilerParams(vmem_limit_bytes=20 * MIB),
    )(*pinned(operands, in_specs))


def halo_stage(north, south, send_rows, edge_in, node_count):
    rows, width = north.shape
    count = send_rows.shape[1]
    in_specs = [VMEM, VMEM, HBM, HBM]
    return pl.pallas_call(
        functools.partial(halo_kernel, node_count),
        out_shape=[jax.ShapeDtypeStruct((2 * rows, width), BF16), pltpu.HBM((count, node_count), BF16)],
        in_specs=in_specs,
        out_specs=[VMEM, HBM],
        scratch_shapes=[
            pltpu.VMEM((1, count), I32), pltpu.VMEM((width, width), BF16),
            pltpu.VMEM((count, node_count), BF16), pltpu.SemaphoreType.DMA((3,)),
        ],
        name="halo_terms",
        cost_estimate=pl.CostEstimate(
            flops=4 * rows * width * width, bytes_accessed=6 * rows * width, transcendentals=0
        ),
        compiler_params=pltpu.CompilerParams(vmem_limit_bytes=8 * MIB),
    )(*pinned([north, south, send_rows, edge_in], in_specs))


def main_stage(level, places, receivers, pre, edges, nodes, weights, tables, picks, last, keep):
    edge_count, width = edges.shape
    node_count = nodes.shape[0]
    operands = [places, receivers, pre, edges, nodes, *weights, *tables]
    in_specs = [HBM] * 12 + [VMEM] * (len(tables) - 1)
    out_shape = [pltpu.HBM((node_count, width), BF16)]
    blocks = edge_count // BLOCK
    table_rows = sum(piece.shape[0] for piece in tables)
    norm = pltpu.VMEM(weights[4].shape, F32)
    small = pltpu.VMEM((node_count, width), BF16)
    weight = pltpu.VMEM((width, width), BF16)
    scratch = [
        pltpu.VMEM((table_rows * (width // LANES), LANES), F32),
        pltpu.VMEM((BLOCK * (width // LANES), LANES), F32),
        pltpu.VMEM((BLOCK * (width // LANES), LANES), F32),
        pltpu.VMEM((BLOCK, width), BF16),
        pltpu.VMEM((BLOCK, width), BF16),
        pltpu.VMEM((BLOCK, width), F32),
        pltpu.VMEM((BLOCK, width), F32),
        pltpu.VMEM((node_count, width), F32),
        pltpu.SMEM((1, edge_count), I32),
        pltpu.VMEM((1, edge_count), I32),
        pltpu.VMEM((edge_count, width), F32),
        pltpu.VMEM((edge_count, width), BF16),
        small, weight, pltpu.VMEM((2, width, width), BF16), weight, norm, norm, small,
        pltpu.VMEM(tables[0].shape, BF16), pltpu.VMEM((edge_count, width), BF16),
    ]
    raw = len(tables) - 2
    if raw:
        scratch.append(weight)
    if not last:
        operands.append(picks)
        in_specs.append(HBM)
        rows = picks.shape[0]
        out_shape += [pltpu.HBM((node_count, width), BF16), pltpu.HBM((rows, width), BF16)]
        scratch += [weight, pltpu.VMEM(picks.shape, BF16), small, pltpu.VMEM((rows, width), BF16)]
    if keep:
        out_shape.append(pltpu.HBM((edge_count, width), BF16))
    scratch += [pltpu.SemaphoreType.DMA((n,)) for n in (14, blocks, blocks, blocks)]
    return pl.pallas_call(
        functools.partial(main_kernel, level, raw, last, keep),
        out_shape=out_shape,
        in_specs=in_specs,
        out_specs=[HBM] * len(out_shape),
        scratch_shapes=scratch,
        name="encode" if level == 0 else "layer",
        cost_estimate=pl.CostEstimate(
            flops=2 * edge_count * width * (width + node_count),
            bytes_accessed=edge_count * width * 10,
            transcendentals=edge_count * width,
        ),
        compiler_params=pltpu.CompilerParams(vmem_limit_bytes=32 * MIB),
    )(*pinned(operands, in_specs))


def shift(array, axis, step, wrap):
    size = lax.axis_size(axis)
    pairs = [(i, (i + step) % size) for i in range(size) if wrap or 0 <= i + step < size]
    return lax.ppermute(array, axis, pairs)


def local(
    grid_latent,
    mesh_latent,
    g2m_edges,
    g2m_senders,
    g2m_receivers,
    mm_edges,
    mm_senders,
    mm_receivers,
    send_rows,
    edge_in,
    edge_out,
    node_in,
    node_out,
    norm_gain,
    norm_bias,
):
    high, wide, features = grid_latent.shape
    flat_tile = grid_latent.reshape(high * wide, features)
    weights = [edge_in, edge_out, node_in, node_out, norm_gain, norm_bias]

    north = shift(grid_latent, "lat", 1, False)
    south = shift(grid_latent, "lat", -1, False)
    pre, tile_terms, places, lines = pre_stage(
        0, g2m_edges, g2m_receivers, mesh_latent, edge_in,
        (flat_tile, g2m_senders, mm_senders), (high, wide),
    )
    north, south, tile_terms = lax.optimization_barrier((north, south, tile_terms))

    def column(first):
        pieces = [piece[:, first:first + HALO] for piece in (north, grid_latent, south)]
        return jnp.concatenate(pieces, axis=0).reshape(-1, features)

    west = shift(column(wide - HALO), "lon", 1, True)
    east = shift(column(0), "lon", -1, True)
    halo_terms, picks = halo_stage(
        north.reshape(-1, features), south.reshape(-1, features), send_rows, edge_in, mesh_latent.shape[0]
    )
    tables = [tile_terms, halo_terms, west, east]
    nodes, outgoing, out_rows = main_stage(
        0, places, g2m_receivers, pre, g2m_edges, mesh_latent, weights, tables, picks, False, False
    )
    edges = mm_edges
    levels = edge_in.shape[0]
    devices = lax.axis_size("lat") * lax.axis_size("lon")
    for level in range(1, levels):
        blocks = out_rows.reshape(devices, -1, features)
        arrived = lax.all_to_all(blocks, ("lat", "lon"), split_axis=0, concat_axis=0, tiled=True)
        arrived = arrived.reshape(-1, features)
        (pre,) = pre_stage(level, edges, mm_receivers, nodes, edge_in)
        last = level == levels - 1
        results = main_stage(
            level, lines, mm_receivers, pre, edges, nodes, weights, [outgoing, arrived], picks,
            last, not last,
        )
        if last:
            (nodes,) = results
        else:
            nodes, outgoing, out_rows, edges = results
    return nodes


def solution(mesh):
    in_specs = (
        P("lat", "lon", None),
        P(("lat", "lon"), None),
        P(("lat", "lon"), None),
        P(("lat", "lon"), None),
        P(("lat", "lon"), None),
        P(("lat", "lon"), None),
        P(("lat", "lon"), None),
        P(("lat", "lon"), None),
        P(("lat", "lon"), None),
        P(),
        P(),
        P(),
        P(),
        P(),
        P(),
    )
    out_specs = P(("lat", "lon"), None)
    return jax.shard_map(local, mesh=mesh, in_specs=in_specs, out_specs=out_specs, check_vma=False)
```

time: 130 us -> 123 us (0.946)
  Pallas kernels: 53.2 us -> 47.2 us
    pallas_call x3, Pallas kernels: 20.2 us -> 16.8 us  [pre_stage(): pl.pallas_call(functools.partial(pre_kernel, level, shape), out_shape=out...]
    pallas_call x3 -> x4, Pallas kernels: 33 us -> 30.4 us  [the longest x3 27 us: main_stage(): pl.pallas_call(functools.partial(main_kernel, level, raw, last, keep), ou...]
    ppermute x4, waiting for transfers between devices: 2 us -> 0.01 us  [shift(): return lax.ppermute(array, axis, pairs)]
  transfers between devices with their start and end apart: 6 -> 6, of which waited for: 3 -> 2; matrix products, arithmetic and copies ran while one was open for 1% -> 1% of each run, Pallas kernels for 16% -> 16%
where the time goes in v3:
time: 123 us
  waiting for transfers between devices  47.8 us (39%)
  Pallas kernels  47.2 us (38%)
  starting transfers between devices  26.6 us (22%)
    all_to_all x2, waiting for transfers between devices, local(): lax.all_to_all(blocks, ('lat', 'lon'), split_axis=0, concat_axis=0, tiled...  47.8 us
    pallas_call x3, Pallas kernels, main_stage(): pl.pallas_call(functools.partial(main_kernel, level, raw, last, keep), ou...  27 us
    all_to_all x2, starting transfers between devices, local(): lax.all_to_all(blocks, ('lat', 'lon'), split_axis=0, concat_axis=0, tiled...  16.8 us
    pallas_call x3, Pallas kernels, pre_stage(): pl.pallas_call(functools.partial(pre_kernel, level, shape), out_shape=out...  16.8 us
    ppermute x4, starting transfers between devices, shift(): return lax.ppermute(array, axis, pairs)  9.81 us
    pallas_call x1, Pallas kernels, halo_stage(): pl.pallas_call(functools.partial(halo_kernel, node_count), out_shape=[jax...  3.46 us
  transfers between devices with their start and end apart: 6, of which 2 were waited for; matrix products, arithmetic and copies ran while one was open for 1% of the time, Pallas kernels for 16%

profile of v3, /device:TPU:0, one launch (start us, length us, event | category | flops | bytes accessed | tf_op | source)
XLA Modules:
  0.0 122.9 jit_solution(2086615942808607857)
XLA Ops:
  0.0 1.3 %collective-permute-start = (bf16[4,128,512]{2,1,0:T(8,128)(2,1)}, bf16[4,128,512]{2,1,0:T(8,128)(2,1)S(1)}, u32[]{:S(2)}, u32[]{:S(2)}) collective-permute-start(bf16[4,128,512]{2,1,0:T(8,128)(2,1)} %param.15), channel_id=1, source_target_pairs={{0,16},{16,32},{32,48},{48,64},{64,80},{80,96},{96,112},{1,17},{17... | collective-permute-start | bytes 1572872 | tf_op jit(solution)/shard_map/ppermute | solution.py:444
  1.3 1.3 %collective-permute-start.1 = (bf16[4,128,512]{2,1,0:T(8,128)(2,1)}, bf16[4,128,512]{2,1,0:T(8,128)(2,1)S(1)}, u32[]{:S(2)}, u32[]{:S(2)}) collective-permute-start(bf16[4,128,512]{2,1,0:T(8,128)(2,1)} %param.15), channel_id=1, source_target_pairs={{16,0},{32,16},{48,32},{64,48},{80,64},{96,80},{112,96},{17,1},{33... | collective-permute-start | bytes 1572872 | tf_op jit(solution)/shard_map/ppermute | solution.py:444
  2.6 5.5 %pre_first.1 = (f32[2048,512]{1,0:T(8,128)}, bf16[512,512]{1,0:T(8,128)(2,1)}, s32[1,2048]{1,0:T(1,128)}, s32[1,2048]{1,0:T(1,128)}) custom-call(bf16[2048,512]{1,0:T(8,128)(2,1)} %refs_3_.2, s32[1,2048]{1,0:T(1,128)} %refs_1_.5, bf16[128,512]{1,0:T(8,128)(2,1)} %refs_4_.1, bf16[3,3,512,512]{3,2,1,0:T(8,128)(2,1)} %refs_5_.5, bf16[512,512]{1,0:T(8,128)(2,1)} %bitcast.13, ...), custom_call_target="tpu_custom_call" | custom-call | flops 1342177280 | bytes 6291456 | tf_op jit(solution)/shard_map/pre_first/pallas_call | solution.py:349
  8.1 0.8 fusion.1
  8.9 0.0 collective-permute-done
  8.9 0.0 collective-permute-done.1
  9.1 2.2 %collective-permute-start.2 = (bf16[48,512]{1,0:T(8,128)(2,1)S(1)}, bf16[48,512]{1,0:T(8,128)(2,1)S(1)}, u32[]{:S(2)}, u32[]{:S(2)}) collective-permute-start(bf16[48,512]{1,0:T(8,128)(2,1)S(1)} %reshape.30), channel_id=1, source_target_pairs={{0,1},{1,2},{2,3},{3,4},{4,5},{5,6},{6,7},{7,8},{8,9},{9,10},{10,1... | collective-permute-start | bytes 147464 | tf_op jit(solution)/shard_map/ppermute | solution.py:444
  11.3 5.0 %collective-permute-start.3 = (bf16[48,512]{1,0:T(8,128)(2,1)S(1)}, bf16[48,512]{1,0:T(8,128)(2,1)S(1)}, u32[]{:S(2)}, u32[]{:S(2)}) collective-permute-start(bf16[48,512]{1,0:T(8,128)(2,1)S(1)} %reshape.31), channel_id=1, source_target_pairs={{0,15},{1,0},{2,1},{3,2},{4,3},{5,4},{6,5},{7,6},{8,7},{9,8},{10,9... | collective-permute-start | bytes 147464 | tf_op jit(solution)/shard_map/ppermute | solution.py:444
  16.3 3.5 %halo_terms.1 = (bf16[1024,512]{1,0:T(8,128)(2,1)S(1)}, bf16[2048,128]{1,0:T(8,128)(2,1)}) custom-call(bf16[512,512]{1,0:T(8,128)(2,1)S(1)} %bitcast.9, bf16[512,512]{1,0:T(8,128)(2,1)S(1)} %bitcast.10, s32[1,2048]{1,0:T(1,128)} %send_rows_h.1, bf16[3,3,512,512]{3,2,1,0:T(8,128)(2,1)} %refs_5_.5), custom_call_target="tpu_custom_call" | custom-call | flops 536870912 | bytes 1572864 | tf_op jit(solution)/shard_map/halo_terms/pallas_call | solution.py:369
  19.7 0.0 collective-permute-done.2.refs_13_
  19.8 0.0 collective-permute-done.3.refs_14_
  19.8 9.4 %encode.1 = (bf16[128,512]{1,0:T(8,128)(2,1)}, bf16[128,512]{1,0:T(8,128)(2,1)}, bf16[2048,512]{1,0:T(8,128)(2,1)}) custom-call(s32[1,2048]{1,0:T(1,128)} %get-tuple-element.22.refs_0_, s32[1,2048]{1,0:T(1,128)} %refs_1_.5, f32[2048,512]{1,0:T(8,128)} %get-tuple-element.23.refs_2_, bf16[2048,512]{1,0:T(8,128)(2,1)} %refs_3_.2, bf16[128,512]{1,0:T(8,128)(2,1)} %refs_4_.1, ...), custom_call_target="tpu_custom_call" | custom-call | flops 1342177280 | bytes 10485760 | tf_op jit(solution)/shard_map/encode/pallas_call | solution.py:425
  29.2 11.9 %all-to-all-start = ((bf16[128,16,512]{2,1,0:T(8,128)(2,1)}), bf16[128,16,512]{2,1,0:T(8,128)(2,1)S(1)}, u32[]{:S(2)}, u32[]{:S(2)}) async-start(bf16[128,16,512]{2,1,0:T(8,128)(2,1)} %bitcast.11), calls=%async_computation | async-start | bytes 4194304 | tf_op jit(solution)/shard_map/all_to_all | solution.py:494
  41.1 5.7 %pre_next.2.refs_2_ = f32[2048,512]{1,0:T(8,128)} custom-call(bf16[2048,512]{1,0:T(8,128)(2,1)} %refs_3_.3, s32[1,2048]{1,0:T(1,128)} %refs_1_.7, bf16[128,512]{1,0:T(8,128)(2,1)} %get-tuple-element.30.nodes_h.refs_4_, bf16[3,3,512,512]{3,2,1,0:T(8,128)(2,1)} %refs_5_.5), custom_call_target="tpu_custom_call" | custom-call | flops 1342177280 | bytes 6291456 | tf_op jit(solution)/shard_map/pre_next/pallas_call | solution.py:349
  46.8 23.9 %all-to-all-done = bf16[128,16,512]{2,1,0:T(8,128)(2,1)S(1)} async-done(((bf16[128,16,512]{2,1,0:T(8,128)(2,1)}), bf16[128,16,512]{2,1,0:T(8,128)(2,1)S(1)}, u32[]{:S(2)}, u32[]{:S(2)}) %all-to-all-start) | async-done | bytes 2097184 | tf_op jit(solution)/shard_map/all_to_all | solution.py:494
  70.7 9.1 %layer.2 = (bf16[128,512]{1,0:T(8,128)(2,1)}, bf16[128,512]{1,0:T(8,128)(2,1)}, bf16[2048,512]{1,0:T(8,128)(2,1)}, bf16[2048,512]{1,0:T(8,128)(2,1)}) custom-call(s32[1,2048]{1,0:T(1,128)} %get-tuple-element.21.refs_0_, s32[1,2048]{1,0:T(1,128)} %refs_1_.7, f32[2048,512]{1,0:T(8,128)} %pre_next.2.refs_2_, bf16[2048,512]{1,0:T(8,128)(2,1)} %refs_3_.3, ...), custom_call_target="tpu_custom_call" | custom-call | flops 1342177280 | bytes 10485760 | tf_op jit(solution)/shard_map/layer/pallas_call | solution.py:425
  79.9 4.9 %all-to-all-start.1 = ((bf16[128,16,512]{2,1,0:T(8,128)(2,1)}), bf16[128,16,512]{2,1,0:T(8,128)(2,1)S(1)}, u32[]{:S(2)}, u32[]{:S(2)}) async-start(bf16[128,16,512]{2,1,0:T(8,128)(2,1)} %bitcast.12), calls=%async_computation.1 | async-start | bytes 4194304 | tf_op jit(solution)/shard_map/all_to_all | solution.py:494
  84.8 5.7 %pre_next.3.refs_2_ = f32[2048,512]{1,0:T(8,128)} custom-call(bf16[2048,512]{1,0:T(8,128)(2,1)} %get-tuple-element.33.edges_h.refs_3_, s32[1,2048]{1,0:T(1,128)} %refs_1_.7, bf16[128,512]{1,0:T(8,128)(2,1)} %get-tuple-element.34.nodes_h.refs_4_, bf16[3,3,512,512]{3,2,1,0:T(8,128)(2,1)} %refs_5_.5), custom_call_target="tpu_custom_call" | custom-call | flops 1342177280 | bytes 6291456 | tf_op jit(solution)/shard_map/pre_next/pallas_call | solution.py:349
  90.4 23.9 %all-to-all-done.1 = bf16[128,16,512]{2,1,0:T(8,128)(2,1)S(1)} async-done(((bf16[128,16,512]{2,1,0:T(8,128)(2,1)}), bf16[128,16,512]{2,1,0:T(8,128)(2,1)S(1)}, u32[]{:S(2)}, u32[]{:S(2)}) %all-to-all-start.1) | async-done | bytes 2097184 | tf_op jit(solution)/shard_map/all_to_all | solution.py:494
  114.3 8.4 %layer.3 = bf16[128,512]{1,0:T(8,128)(2,1)} custom-call(s32[1,2048]{1,0:T(1,128)} %get-tuple-element.21.refs_0_, s32[1,2048]{1,0:T(1,128)} %refs_1_.7, f32[2048,512]{1,0:T(8,128)} %pre_next.3.refs_2_, bf16[2048,512]{1,0:T(8,128)(2,1)} %get-tuple-element.33.edges_h.refs_3_, bf16[128,512]{1,0:T(8,128)(2,1)} %get-tuple-element.34.nodes_h.refs_4_, ...), custom_call_target="tpu_custom_call" | custom-call | flops 1342177280 | bytes 10485760 | tf_op jit(solution)/shard_map/layer/pallas_call | solution.py:425
  (5 shorter events, 0.1 us)
Async XLA Ops:
  0.0 8.9 %collective-permute-start = (bf16[4,128,512]{2,1,0:T(8,128)(2,1)}, bf16[4,128,512]{2,1,0:T(8,128)(2,1)S(1)}, u32[]{:S(2)}, u32[]{:S(2)}) collective-permute-start(bf16[4,128,512]{2,1,0:T(8,128)(2,1)} %param.15), channel_id=1, source_target_pairs={{0,16},{16,32},{32,48},{48,64},{64,80},{80,96},{96,112},{1,17},{17... | collective-permute-start | bytes 1572872 | tf_op jit(solution)/shard_map/ppermute | solution.py:444
  1.3 7.6 %collective-permute-start.1 = (bf16[4,128,512]{2,1,0:T(8,128)(2,1)}, bf16[4,128,512]{2,1,0:T(8,128)(2,1)S(1)}, u32[]{:S(2)}, u32[]{:S(2)}) collective-permute-start(bf16[4,128,512]{2,1,0:T(8,128)(2,1)} %param.15), channel_id=1, source_target_pairs={{16,0},{32,16},{48,32},{64,48},{80,64},{96,80},{112,96},{17,1},{33... | collective-permute-start | bytes 1572872 | tf_op jit(solution)/shard_map/ppermute | solution.py:444
  9.1 10.7 %collective-permute-start.2 = (bf16[48,512]{1,0:T(8,128)(2,1)S(1)}, bf16[48,512]{1,0:T(8,128)(2,1)S(1)}, u32[]{:S(2)}, u32[]{:S(2)}) collective-permute-start(bf16[48,512]{1,0:T(8,128)(2,1)S(1)} %reshape.30), channel_id=1, source_target_pairs={{0,1},{1,2},{2,3},{3,4},{4,5},{5,6},{6,7},{7,8},{8,9},{9,10},{10,1... | collective-permute-start | bytes 147464 | tf_op jit(solution)/shard_map/ppermute | solution.py:444
  11.3 8.5 %collective-permute-start.3 = (bf16[48,512]{1,0:T(8,128)(2,1)S(1)}, bf16[48,512]{1,0:T(8,128)(2,1)S(1)}, u32[]{:S(2)}, u32[]{:S(2)}) collective-permute-start(bf16[48,512]{1,0:T(8,128)(2,1)S(1)} %reshape.31), channel_id=1, source_target_pairs={{0,15},{1,0},{2,1},{3,2},{4,3},{5,4},{6,5},{7,6},{8,7},{9,8},{10,9... | collective-permute-start | bytes 147464 | tf_op jit(solution)/shard_map/ppermute | solution.py:444
  29.2 41.5 %all-to-all-start = ((bf16[128,16,512]{2,1,0:T(8,128)(2,1)}), bf16[128,16,512]{2,1,0:T(8,128)(2,1)S(1)}, u32[]{:S(2)}, u32[]{:S(2)}) async-start(bf16[128,16,512]{2,1,0:T(8,128)(2,1)} %bitcast.11), calls=%async_computation | async-start | bytes 4194304 | tf_op jit(solution)/shard_map/all_to_all | solution.py:494
  79.9 34.4 %all-to-all-start.1 = ((bf16[128,16,512]{2,1,0:T(8,128)(2,1)}), bf16[128,16,512]{2,1,0:T(8,128)(2,1)S(1)}, u32[]{:S(2)}, u32[]{:S(2)}) async-start(bf16[128,16,512]{2,1,0:T(8,128)(2,1)} %bitcast.12), calls=%async_computation.1 | async-start | bytes 4194304 | tf_op jit(solution)/shard_map/all_to_all | solution.py:494

commit v4 on v3

--- a/solution.py
+++ b/solution.py
@@ -12,10 +12,11 @@
 F32 = jnp.float32
 BF16 = jnp.bfloat16
 I32 = jnp.int32
-BLOCK = 256
+BLOCK = 512
 CHUNK = 256
-GROUP = 16
+GROUP = 32
 PRE_BLOCK = 512
+PICK_BLOCK = 256
 LANES = 128
 MIB = 1024 * 1024
 
@@ -77,13 +78,13 @@
     refs = list(refs)
     take = lambda count: [refs.pop(0) for _ in range(count)]
     if shape:
-        tile_h, cells_h, senders_h = take(3)
+        tile_h, cells_h, senders_h, send_rows_h = take(4)
     pre_h = take(1)[0]
     if shape:
-        tile_terms_h, places_h, lines_h = take(3)
+        tile_terms_h, places_h, lines_h, picks_h = take(4)
     edges, receivers, nodes, w_edge, w_recv, pre = take(6)
     if shape:
-        tile, w_send, cells, senders, tile_terms, places, lines = take(7)
+        tile, w_send, cells, senders, tile_terms, places, lines, send_rows, picks = take(9)
     sems, edge_sems, out_sems = take(3)
     node_count = nodes.shape[0]
     blocks = edges.shape[0] // PRE_BLOCK
@@ -107,6 +108,7 @@
             begin(edge_in_h.at[level, 1], w_send, sems.at[5]),
             begin(cells_h, cells, sems.at[6]),
             begin(senders_h, senders, sems.at[7]),
+            begin(send_rows_h, send_rows, sems.at[11]),
         ]
     for i in range(1, blocks):
         edge_copy(i).start()
@@ -128,12 +130,20 @@
         tiles = edges.shape[1] // LANES
         for copy in second:
             copy.wait()
+
+        def pick(i, _):
+            rows = pl.ds(pl.multiple_of(i * PRE_BLOCK, PRE_BLOCK), PRE_BLOCK)
+            picks[rows, :] = hot_rows(send_rows[:, rows], node_count)
+            return 0
+
+        lax.fori_loop(0, picks.shape[0] // PRE_BLOCK, pick, 0)
         tile_terms[...] = project(tile[...], w_send[...])
         ends = [begin(tile_terms, tile_terms_h, sems.at[8])]
         places[...] = cell_row(cells[...], high, wide) * tiles
         lines[...] = senders[...] * tiles
         ends.append(begin(places, places_h, sems.at[9]))
         ends.append(begin(lines, lines_h, sems.at[10]))
+        ends.append(begin(picks, picks_h, sems.at[12]))
     for i in range(blocks):
         out_copy(i).wait()
     if shape:
@@ -141,24 +151,11 @@
             copy.wait()
 
 
-def halo_kernel(node_count, north, south, send_rows_h, edge_in_h, terms, picks_h, send_rows, w_send, picks, sems):
-    copies = [
-        begin(edge_in_h.at[0, 1], w_send, sems.at[0]),
-        begin(send_rows_h, send_rows, sems.at[1]),
-    ]
-    for copy in copies:
-        copy.wait()
+def halo_kernel(north, south, edge_in_h, terms, w_send, sem):
+    begin(edge_in_h.at[0, 1], w_send, sem).wait()
     size = north.shape[0]
     terms[0:size, :] = project(north[...], w_send[...])
     terms[size:2 * size, :] = project(south[...], w_send[...])
-
-    def pick(i, _):
-        rows = pl.ds(pl.multiple_of(i * BLOCK, BLOCK), BLOCK)
-        picks[rows, :] = hot_rows(send_rows[:, rows], node_count)
-        return 0
-
-    lax.fori_loop(0, picks.shape[0] // BLOCK, pick, 0)
-    begin(picks, picks_h, sems.at[2]).wait()
 
 
 def fill_table(table, start, values):
@@ -185,7 +182,7 @@
     nodes, w_out, w_node, w_node_out, gain, bias, new_nodes, local_rows, fresh_edges = take(9)
     w_send = take(1)[0] if raw else None
     w_next, picks, outgoing, out_rows = (None,) * 4 if last else take(4)
-    sems, pre_sems, edge_sems, out_sems = take(4)
+    sems, pre_sems, edge_sems, out_sems, pick_sems = take(5)
 
     node_count, width = nodes.shape
     blocks = edges.shape[0] // BLOCK
@@ -305,10 +302,10 @@
         sent = project(updated, w_next[...])
         outgoing[...] = sent
         ends.append(begin(outgoing, outgoing_h, sems.at[13]))
-        for i in range(out_rows.shape[0] // BLOCK):
-            rows = pl.ds(i * BLOCK, BLOCK)
+        for i in range(out_rows.shape[0] // PICK_BLOCK):
+            rows = pl.ds(i * PICK_BLOCK, PICK_BLOCK)
             out_rows[rows, :] = dot(picks[rows, :], sent).astype(BF16)
-            ends.append(begin(out_rows.at[rows], out_rows_h.at[rows], pre_sems.at[i]))
+            ends.append(begin(out_rows.at[rows], out_rows_h.at[rows], pick_sems.at[i]))
     if keep:
         for i in range(blocks):
             fresh_copy(i).wait()
@@ -341,10 +338,12 @@
         tile = extra[0]
         out_shape += [
             pltpu.HBM(tile.shape, BF16), pltpu.HBM((1, edge_count), I32), pltpu.HBM((1, edge_count), I32),
+            pltpu.HBM((edge_count, node_count), BF16),
         ]
         tiled = pltpu.VMEM(tile.shape, BF16)
-        scratch += [tiled, weight, line, line, tiled, line, line]
-    scratch += [pltpu.SemaphoreType.DMA((n,)) for n in (11, blocks, blocks)]
+        scratch += [tiled, weight, line, line, tiled, line, line, line]
+        scratch.append(pltpu.VMEM((edge_count, node_count), BF16))
+    scratch += [pltpu.SemaphoreType.DMA((n,)) for n in (13, blocks, blocks)]
     in_specs = [HBM] * len(operands)
     return pl.pallas_call(
         functools.partial(pre_kernel, level, shape),
@@ -362,25 +361,21 @@
     )(*pinned(operands, in_specs))
 
 
-def halo_stage(north, south, send_rows, edge_in, node_count):
+def halo_stage(north, south, edge_in):
     rows, width = north.shape
-    count = send_rows.shape[1]
-    in_specs = [VMEM, VMEM, HBM, HBM]
+    in_specs = [VMEM, VMEM, HBM]
     return pl.pallas_call(
-        functools.partial(halo_kernel, node_count),
-        out_shape=[jax.ShapeDtypeStruct((2 * rows, width), BF16), pltpu.HBM((count, node_count), BF16)],
+        halo_kernel,
+        out_shape=jax.ShapeDtypeStruct((2 * rows, width), BF16),
         in_specs=in_specs,
-        out_specs=[VMEM, HBM],
-        scratch_shapes=[
-            pltpu.VMEM((1, count), I32), pltpu.VMEM((width, width), BF16),
-            pltpu.VMEM((count, node_count), BF16), pltpu.SemaphoreType.DMA((3,)),
-        ],
+        out_specs=VMEM,
+        scratch_shapes=[pltpu.VMEM((width, width), BF16), pltpu.SemaphoreType.DMA],
         name="halo_terms",
         cost_estimate=pl.CostEstimate(
             flops=4 * rows * width * width, bytes_accessed=6 * rows * width, transcendentals=0
         ),
         compiler_params=pltpu.CompilerParams(vmem_limit_bytes=8 * MIB),
-    )(*pinned([north, south, send_rows, edge_in], in_specs))
+    )(*pinned([north, south, edge_in], in_specs))
 
 
 def main_stage(level, places, receivers, pre, edges, nodes, weights, tables, picks, last, keep):
@@ -421,7 +416,7 @@
         scratch += [weight, pltpu.VMEM(picks.shape, BF16), small, pltpu.VMEM((rows, width), BF16)]
     if keep:
         out_shape.append(pltpu.HBM((edge_count, width), BF16))
-    scratch += [pltpu.SemaphoreType.DMA((n,)) for n in (14, blocks, blocks, blocks)]
+    scratch += [pltpu.SemaphoreType.DMA((n,)) for n in (14, blocks, blocks, blocks, edge_count // PICK_BLOCK)]
     return pl.pallas_call(
         functools.partial(main_kernel, level, raw, last, keep),
         out_shape=out_shape,
@@ -467,9 +462,9 @@
 
     north = shift(grid_latent, "lat", 1, False)
     south = shift(grid_latent, "lat", -1, False)
-    pre, tile_terms, places, lines = pre_stage(
+    pre, tile_terms, places, lines, picks = pre_stage(
         0, g2m_edges, g2m_receivers, mesh_latent, edge_in,
-        (flat_tile, g2m_senders, mm_senders), (high, wide),
+        (flat_tile, g2m_senders, mm_senders, send_rows), (high, wide),
     )
     north, south, tile_terms = lax.optimization_barrier((north, south, tile_terms))
 
@@ -479,9 +474,7 @@
 
     west = shift(column(wide - HALO), "lon", 1, True)
     east = shift(column(0), "lon", -1, True)
-    halo_terms, picks = halo_stage(
-        north.reshape(-1, features), south.reshape(-1, features), send_rows, edge_in, mesh_latent.shape[0]
-    )
+    halo_terms = halo_stage(north.reshape(-1, features), south.reshape(-1, features), edge_in)
     tables = [tile_terms, halo_terms, west, east]
     nodes, outgoing, out_rows = main_stage(
         0, places, g2m_receivers, pre, g2m_edges, mesh_latent, weights, tables, picks, False, False

time: 123 us -> 123 us (level)
  Pallas kernels: 47.2 us -> 45.4 us
    pallas_call x1, Pallas kernels: 3.46 us -> 1.76 us  [halo_stage(): pl.pallas_call(halo_kernel, out_shape=jax.ShapeDtypeStruct((2 * rows, wid...]
  transfers between devices with their start and end apart: 6 -> 6, of which waited for: 2 -> 3; matrix products, arithmetic and copies ran while one was open for 1% -> 1% of each run, Pallas kernels for 16% -> 16%
where the time goes in v4:
time: 123 us; the launch traced here: 122 us
  waiting for transfers between devices  48.2 us (39%)
  Pallas kernels  45.4 us (37%)
  starting transfers between devices  27.2 us (22%)
    all_to_all x2, waiting for transfers between devices, local(): lax.all_to_all(blocks, ('lat', 'lon'), split_axis=0, concat_axis=0, tiled...  48 us
    pallas_call x3, Pallas kernels, main_stage(): pl.pallas_call(functools.partial(main_kernel, level, raw, last, keep), ou...  26.2 us
    pallas_call x3, Pallas kernels, pre_stage(): pl.pallas_call(functools.partial(pre_kernel, level, shape), out_shape=out...  17.5 us
    all_to_all x2, starting transfers between devices, local(): lax.all_to_all(blocks, ('lat', 'lon'), split_axis=0, concat_axis=0, tiled...  17.4 us
    ppermute x4, starting transfers between devices, shift(): return lax.ppermute(array, axis, pairs)  9.81 us
  transfers between devices with their start and end apart: 6, of which 3 were waited for; matrix products, arithmetic and copies ran while one was open for 1% of the time, Pallas kernels for 16%

profile of v4, /device:TPU:0, one launch (start us, length us, event | category | flops | bytes accessed | tf_op | source)
XLA Modules:
  0.0 122.1 jit_solution(16767071197446361885)
XLA Ops:
  0.0 1.3 %collective-permute-start = (bf16[4,128,512]{2,1,0:T(8,128)(2,1)}, bf16[4,128,512]{2,1,0:T(8,128)(2,1)S(1)}, u32[]{:S(2)}, u32[]{:S(2)}) collective-permute-start(bf16[4,128,512]{2,1,0:T(8,128)(2,1)} %param.15), channel_id=1, source_target_pairs={{0,16},{16,32},{32,48},{48,64},{64,80},{80,96},{96,112},{1,17},{17... | collective-permute-start | bytes 1572872 | tf_op jit(solution)/shard_map/ppermute | solution.py:439
  1.3 1.3 %collective-permute-start.1 = (bf16[4,128,512]{2,1,0:T(8,128)(2,1)}, bf16[4,128,512]{2,1,0:T(8,128)(2,1)S(1)}, u32[]{:S(2)}, u32[]{:S(2)}) collective-permute-start(bf16[4,128,512]{2,1,0:T(8,128)(2,1)} %param.15), channel_id=1, source_target_pairs={{16,0},{32,16},{48,32},{64,48},{80,64},{96,80},{112,96},{17,1},{33... | collective-permute-start | bytes 1572872 | tf_op jit(solution)/shard_map/ppermute | solution.py:439
  2.6 6.1 %pre_first.1 = (f32[2048,512]{1,0:T(8,128)}, bf16[512,512]{1,0:T(8,128)(2,1)}, s32[1,2048]{1,0:T(1,128)}, s32[1,2048]{1,0:T(1,128)}, bf16[2048,128]{1,0:T(8,128)(2,1)}) custom-call(bf16[2048,512]{1,0:T(8,128)(2,1)} %refs_3_.4, s32[1,2048]{1,0:T(1,128)} %refs_1_.5, bf16[128,512]{1,0:T(8,128)(2,1)} %refs_4_.1, bf16[3,3,512,512]{3,2,1,0:T(8,128)(2,1)} %refs_5_.5, ...), custom_call_target="tpu_custom_call" | custom-call | flops 1342177280 | bytes 6291456 | tf_op jit(solution)/shard_map/pre_first/pallas_call | solution.py:348
  8.8 0.8 fusion.1
  9.6 0.0 collective-permute-done
  9.6 0.0 collective-permute-done.1
  9.8 2.2 %collective-permute-start.2 = (bf16[48,512]{1,0:T(8,128)(2,1)S(1)}, bf16[48,512]{1,0:T(8,128)(2,1)S(1)}, u32[]{:S(2)}, u32[]{:S(2)}) collective-permute-start(bf16[48,512]{1,0:T(8,128)(2,1)S(1)} %reshape.30), channel_id=1, source_target_pairs={{0,1},{1,2},{2,3},{3,4},{4,5},{5,6},{6,7},{7,8},{8,9},{9,10},{10,1... | collective-permute-start | bytes 147464 | tf_op jit(solution)/shard_map/ppermute | solution.py:439
  12.0 5.0 %collective-permute-start.3 = (bf16[48,512]{1,0:T(8,128)(2,1)S(1)}, bf16[48,512]{1,0:T(8,128)(2,1)S(1)}, u32[]{:S(2)}, u32[]{:S(2)}) collective-permute-start(bf16[48,512]{1,0:T(8,128)(2,1)S(1)} %reshape.31), channel_id=1, source_target_pairs={{0,15},{1,0},{2,1},{3,2},{4,3},{5,4},{6,5},{7,6},{8,7},{9,8},{10,9... | collective-permute-start | bytes 147464 | tf_op jit(solution)/shard_map/ppermute | solution.py:439
  17.0 1.8 %halo_terms.1.refs_12_ = bf16[1024,512]{1,0:T(8,128)(2,1)S(1)} custom-call(bf16[512,512]{1,0:T(8,128)(2,1)S(1)} %bitcast.9, bf16[512,512]{1,0:T(8,128)(2,1)S(1)} %bitcast.10, bf16[3,3,512,512]{3,2,1,0:T(8,128)(2,1)} %refs_5_.5), custom_call_target="tpu_custom_call" | custom-call | flops 536870912 | bytes 1572864 | tf_op jit(solution)/shard_map/halo_terms/pallas_call | solution.py:367
  18.7 0.2 collective-permute-done.2.refs_13_
  19.0 0.0 collective-permute-done.3.refs_14_
  19.0 9.3 %encode.1 = (bf16[128,512]{1,0:T(8,128)(2,1)}, bf16[128,512]{1,0:T(8,128)(2,1)}, bf16[2048,512]{1,0:T(8,128)(2,1)}) custom-call(s32[1,2048]{1,0:T(1,128)} %get-tuple-element.21.refs_0_, s32[1,2048]{1,0:T(1,128)} %refs_1_.5, f32[2048,512]{1,0:T(8,128)} %get-tuple-element.22.refs_2_, bf16[2048,512]{1,0:T(8,128)(2,1)} %refs_3_.4, bf16[128,512]{1,0:T(8,128)(2,1)} %refs_4_.1, ...), custom_call_target="tpu_custom_call" | custom-call | flops 1342177280 | bytes 10485760 | tf_op jit(solution)/shard_map/encode/pallas_call | solution.py:420
  28.3 12.7 %all-to-all-start = ((bf16[128,16,512]{2,1,0:T(8,128)(2,1)}), bf16[128,16,512]{2,1,0:T(8,128)(2,1)S(1)}, u32[]{:S(2)}, u32[]{:S(2)}) async-start(bf16[128,16,512]{2,1,0:T(8,128)(2,1)} %bitcast.11), calls=%async_computation | async-start | bytes 4194304 | tf_op jit(solution)/shard_map/all_to_all | solution.py:487
  41.0 5.7 %pre_next.2.refs_2_ = f32[2048,512]{1,0:T(8,128)} custom-call(bf16[2048,512]{1,0:T(8,128)(2,1)} %refs_3_.5, s32[1,2048]{1,0:T(1,128)} %refs_1_.7, bf16[128,512]{1,0:T(8,128)(2,1)} %get-tuple-element.28.nodes_h.refs_4_, bf16[3,3,512,512]{3,2,1,0:T(8,128)(2,1)} %refs_5_.5), custom_call_target="tpu_custom_call" | custom-call | flops 1342177280 | bytes 6291456 | tf_op jit(solution)/shard_map/pre_next/pallas_call | solution.py:348
  46.7 23.9 %all-to-all-done = bf16[128,16,512]{2,1,0:T(8,128)(2,1)S(1)} async-done(((bf16[128,16,512]{2,1,0:T(8,128)(2,1)}), bf16[128,16,512]{2,1,0:T(8,128)(2,1)S(1)}, u32[]{:S(2)}, u32[]{:S(2)}) %all-to-all-start) | async-done | bytes 2097184 | tf_op jit(solution)/shard_map/all_to_all | solution.py:487
  70.6 9.2 %layer.2 = (bf16[128,512]{1,0:T(8,128)(2,1)}, bf16[128,512]{1,0:T(8,128)(2,1)}, bf16[2048,512]{1,0:T(8,128)(2,1)}, bf16[2048,512]{1,0:T(8,128)(2,1)}) custom-call(s32[1,2048]{1,0:T(1,128)} %get-tuple-element.20.refs_0_, s32[1,2048]{1,0:T(1,128)} %refs_1_.7, f32[2048,512]{1,0:T(8,128)} %pre_next.2.refs_2_, bf16[2048,512]{1,0:T(8,128)(2,1)} %refs_3_.5, ...), custom_call_target="tpu_custom_call" | custom-call | flops 1342177280 | bytes 10485760 | tf_op jit(solution)/shard_map/layer/pallas_call | solution.py:420
  79.9 4.7 %all-to-all-start.1 = ((bf16[128,16,512]{2,1,0:T(8,128)(2,1)}), bf16[128,16,512]{2,1,0:T(8,128)(2,1)S(1)}, u32[]{:S(2)}, u32[]{:S(2)}) async-start(bf16[128,16,512]{2,1,0:T(8,128)(2,1)} %bitcast.12), calls=%async_computation.1 | async-start | bytes 4194304 | tf_op jit(solution)/shard_map/all_to_all | solution.py:487
  84.5 5.7 %pre_next.3.refs_2_ = f32[2048,512]{1,0:T(8,128)} custom-call(bf16[2048,512]{1,0:T(8,128)(2,1)} %get-tuple-element.31.edges_h.refs_3_, s32[1,2048]{1,0:T(1,128)} %refs_1_.7, bf16[128,512]{1,0:T(8,128)(2,1)} %get-tuple-element.32.nodes_h.refs_4_, bf16[3,3,512,512]{3,2,1,0:T(8,128)(2,1)} %refs_5_.5), custom_call_target="tpu_custom_call" | custom-call | flops 1342177280 | bytes 6291456 | tf_op jit(solution)/shard_map/pre_next/pallas_call | solution.py:348
  90.2 24.1 %all-to-all-done.1 = bf16[128,16,512]{2,1,0:T(8,128)(2,1)S(1)} async-done(((bf16[128,16,512]{2,1,0:T(8,128)(2,1)}), bf16[128,16,512]{2,1,0:T(8,128)(2,1)S(1)}, u32[]{:S(2)}, u32[]{:S(2)}) %all-to-all-start.1) | async-done | bytes 2097184 | tf_op jit(solution)/shard_map/all_to_all | solution.py:487
  114.3 7.7 %layer.3 = bf16[128,512]{1,0:T(8,128)(2,1)} custom-call(s32[1,2048]{1,0:T(1,128)} %get-tuple-element.20.refs_0_, s32[1,2048]{1,0:T(1,128)} %refs_1_.7, f32[2048,512]{1,0:T(8,128)} %pre_next.3.refs_2_, bf16[2048,512]{1,0:T(8,128)(2,1)} %get-tuple-element.31.edges_h.refs_3_, bf16[128,512]{1,0:T(8,128)(2,1)} %get-tuple-element.32.nodes_h.refs_4_, ...), custom_call_target="tpu_custom_call" | custom-call | flops 1342177280 | bytes 10485760 | tf_op jit(solution)/shard_map/layer/pallas_call | solution.py:420
  (5 shorter events, 0.1 us)
Async XLA Ops:
  0.0 9.6 %collective-permute-start = (bf16[4,128,512]{2,1,0:T(8,128)(2,1)}, bf16[4,128,512]{2,1,0:T(8,128)(2,1)S(1)}, u32[]{:S(2)}, u32[]{:S(2)}) collective-permute-start(bf16[4,128,512]{2,1,0:T(8,128)(2,1)} %param.15), channel_id=1, source_target_pairs={{0,16},{16,32},{32,48},{48,64},{64,80},{80,96},{96,112},{1,17},{17... | collective-permute-start | bytes 1572872 | tf_op jit(solution)/shard_map/ppermute | solution.py:439
  1.3 8.3 %collective-permute-start.1 = (bf16[4,128,512]{2,1,0:T(8,128)(2,1)}, bf16[4,128,512]{2,1,0:T(8,128)(2,1)S(1)}, u32[]{:S(2)}, u32[]{:S(2)}) collective-permute-start(bf16[4,128,512]{2,1,0:T(8,128)(2,1)} %param.15), channel_id=1, source_target_pairs={{16,0},{32,16},{48,32},{64,48},{80,64},{96,80},{112,96},{17,1},{33... | collective-permute-start | bytes 1572872 | tf_op jit(solution)/shard_map/ppermute | solution.py:439
  9.8 9.2 %collective-permute-start.2 = (bf16[48,512]{1,0:T(8,128)(2,1)S(1)}, bf16[48,512]{1,0:T(8,128)(2,1)S(1)}, u32[]{:S(2)}, u32[]{:S(2)}) collective-permute-start(bf16[48,512]{1,0:T(8,128)(2,1)S(1)} %reshape.30), channel_id=1, source_target_pairs={{0,1},{1,2},{2,3},{3,4},{4,5},{5,6},{6,7},{7,8},{8,9},{9,10},{10,1... | collective-permute-start | bytes 147464 | tf_op jit(solution)/shard_map/ppermute | solution.py:439
  12.0 7.0 %collective-permute-start.3 = (bf16[48,512]{1,0:T(8,128)(2,1)S(1)}, bf16[48,512]{1,0:T(8,128)(2,1)S(1)}, u32[]{:S(2)}, u32[]{:S(2)}) collective-permute-start(bf16[48,512]{1,0:T(8,128)(2,1)S(1)} %reshape.31), channel_id=1, source_target_pairs={{0,15},{1,0},{2,1},{3,2},{4,3},{5,4},{6,5},{7,6},{8,7},{9,8},{10,9... | collective-permute-start | bytes 147464 | tf_op jit(solution)/shard_map/ppermute | solution.py:439
  28.3 42.4 %all-to-all-start = ((bf16[128,16,512]{2,1,0:T(8,128)(2,1)}), bf16[128,16,512]{2,1,0:T(8,128)(2,1)S(1)}, u32[]{:S(2)}, u32[]{:S(2)}) async-start(bf16[128,16,512]{2,1,0:T(8,128)(2,1)} %bitcast.11), calls=%async_computation | async-start | bytes 4194304 | tf_op jit(solution)/shard_map/all_to_all | solution.py:487
  79.9 34.4 %all-to-all-start.1 = ((bf16[128,16,512]{2,1,0:T(8,128)(2,1)}), bf16[128,16,512]{2,1,0:T(8,128)(2,1)S(1)}, u32[]{:S(2)}, u32[]{:S(2)}) async-start(bf16[128,16,512]{2,1,0:T(8,128)(2,1)} %bitcast.12), calls=%async_computation.1 | async-start | bytes 4194304 | tf_op jit(solution)/shard_map/all_to_all | solution.py:487

commit v5 on v4

--- a/solution.py
+++ b/solution.py
@@ -12,7 +12,9 @@
 F32 = jnp.float32
 BF16 = jnp.bfloat16
 I32 = jnp.int32
-BLOCK = 512
+SIZES = (256, 512, 512, 512, 256)
+STARTS = tuple(sum(SIZES[:i]) for i in range(len(SIZES)))
+BLOCK = max(SIZES)
 CHUNK = 256
 GROUP = 32
 PRE_BLOCK = 512
@@ -70,7 +72,11 @@
     return copy
 
 
-def part(ref, i, size=BLOCK):
+def piece(ref, i):
+    return ref.at[pl.ds(STARTS[i], SIZES[i])]
+
+
+def part(ref, i, size):
     return ref.at[pl.ds(pl.multiple_of(i * size, size), size)]
 
 
@@ -185,20 +191,20 @@
     sems, pre_sems, edge_sems, out_sems, pick_sems = take(5)
 
     node_count, width = nodes.shape
-    blocks = edges.shape[0] // BLOCK
+    blocks = len(SIZES)
     tiles = width // LANES
     stages = [stage_0, stage_1]
     hidden = [hidden_0, hidden_1]
     outputs = [output_0, output_1]
 
     def pre_copy(i):
-        return pltpu.make_async_copy(part(pre_h, i), part(pre, i), pre_sems.at[i])
+        return pltpu.make_async_copy(piece(pre_h, i), piece(pre, i), pre_sems.at[i])
 
     def edge_copy(i):
-        return pltpu.make_async_copy(part(edges_h, i), part(edges, i), edge_sems.at[i])
+        return pltpu.make_async_copy(piece(edges_h, i), piece(edges, i), edge_sems.at[i])
 
     def fresh_copy(i):
-        return pltpu.make_async_copy(part(fresh_edges, i), part(new_edges_h, i), out_sems.at[i])
+        return pltpu.make_async_copy(piece(fresh_edges, i), piece(new_edges_h, i), out_sems.at[i])
 
     places_copy = begin(places_h, places, sems.at[1])
     local_copy = begin(local_h, local_rows, sems.at[0])
@@ -239,17 +245,18 @@
         start += source.shape[0]
     places_copy.wait()
 
-    def found(at):
-        stage = stages[at // BLOCK % 2]
-        base = at % BLOCK * tiles
+    def found(i, at):
+        stage = stages[i % 2]
+        base = (at - STARTS[i]) * tiles
         for j in range(8):
             stage[base + j * tiles:base + (j + 1) * tiles, :] = table[pl.ds(places[0, at + j], tiles), :]
         return [stage[pl.ds(base + tile, 8, stride=tiles), :] for tile in range(tiles)]
 
     def gather(i, group):
         halves = []
-        for at in range(i * BLOCK + group * GROUP, i * BLOCK + (group + 1) * GROUP, 8):
-            rows = found(at)
+        first = STARTS[i] + group * GROUP
+        for at in range(first, first + GROUP, 8):
+            rows = found(i, at)
             halves.append([
                 silu_of_half(pre[at:at + 8, t * LANES:(t + 1) * LANES] + rows[t]) for t in range(tiles)
             ])
@@ -258,7 +265,7 @@
             hidden[i % 2][group * GROUP:(group + 1) * GROUP, t * LANES:(t + 1) * LANES] = both
 
     def settle(i, group):
-        rows = slice(i * BLOCK + group * GROUP, i * BLOCK + (group + 1) * GROUP)
+        rows = slice(STARTS[i] + group * GROUP, STARTS[i] + (group + 1) * GROUP)
         output = outputs[i % 2][group * GROUP:(group + 1) * GROUP, :]
         fresh = normalize(output, gain[level, 0:1, :], bias[level, 0:1, :])
         fresh_edges[rows, :] = (edges[rows, :].astype(F32) + fresh).astype(BF16)
@@ -278,15 +285,16 @@
         if keep and adding is not None:
             fresh_copy(adding).start()
         if multiplying is not None:
-            outputs[multiplying % 2][...] = dot(hidden[multiplying % 2][...], w_out[...])
+            size = SIZES[multiplying]
+            outputs[multiplying % 2][0:size, :] = dot(hidden[multiplying % 2][0:size, :], w_out[...])
         if adding is not None:
-            rows = slice(adding * BLOCK, (adding + 1) * BLOCK)
+            rows = slice(STARTS[adding], STARTS[adding] + SIZES[adding])
             hot = hot_columns(receivers[:, rows], node_count).astype(BF16)
             total[...] += dot(hot, fresh_edges[rows, :])
         for group in range(BLOCK // GROUP):
-            if gathering is not None:
+            if gathering is not None and group < SIZES[gathering] // GROUP:
                 gather(gathering, group)
-            if settling is not None:
+            if settling is not None and group < SIZES[settling] // GROUP:
                 settle(settling, group)
 
     for copy in third:
@@ -384,7 +392,7 @@
     operands = [places, receivers, pre, edges, nodes, *weights, *tables]
     in_specs = [HBM] * 12 + [VMEM] * (len(tables) - 1)
     out_shape = [pltpu.HBM((node_count, width), BF16)]
-    blocks = edge_count // BLOCK
+    blocks = len(SIZES)
     table_rows = sum(piece.shape[0] for piece in tables)
     norm = pltpu.VMEM(weights[4].shape, F32)
     small = pltpu.VMEM((node_count, width), BF16)

time: 123 us -> 122 us (level)
  no operation moved by 1% of the time
where the time goes in v5:
time: 122 us
  waiting for transfers between devices  48.2 us (40%)
  Pallas kernels  45.4 us (37%)
  starting transfers between devices  27.2 us (22%)
    all_to_all x2, waiting for transfers between devices, local(): lax.all_to_all(blocks, ('lat', 'lon'), split_axis=0, concat_axis=0, tiled...  48 us
    pallas_call x3, Pallas kernels, main_stage(): pl.pallas_call(functools.partial(main_kernel, level, raw, last, keep), ou...  26.1 us
    pallas_call x3, Pallas kernels, pre_stage(): pl.pallas_call(functools.partial(pre_kernel, level, shape), out_shape=out...  17.5 us
    all_to_all x2, starting transfers between devices, local(): lax.all_to_all(blocks, ('lat', 'lon'), split_axis=0, concat_axis=0, tiled...  17.4 us
    ppermute x4, starting transfers between devices, shift(): return lax.ppermute(array, axis, pairs)  9.81 us
  transfers between devices with their start and end apart: 6, of which 3 were waited for; matrix products, arithmetic and copies ran while one was open for 1% of the time, Pallas kernels for 16%

profile of v5, /device:TPU:0, one launch (start us, length us, event | category | flops | bytes accessed | tf_op | source)
XLA Modules:
  0.0 122.1 jit_solution(13434148168399004020)
XLA Ops:
  0.0 1.3 %collective-permute-start = (bf16[4,128,512]{2,1,0:T(8,128)(2,1)}, bf16[4,128,512]{2,1,0:T(8,128)(2,1)S(1)}, u32[]{:S(2)}, u32[]{:S(2)}) collective-permute-start(bf16[4,128,512]{2,1,0:T(8,128)(2,1)} %param.15), channel_id=1, source_target_pairs={{0,16},{16,32},{32,48},{48,64},{64,80},{80,96},{96,112},{1,17},{17... | collective-permute-start | bytes 1572872 | tf_op jit(solution)/shard_map/ppermute | solution.py:447
  1.3 1.3 %collective-permute-start.1 = (bf16[4,128,512]{2,1,0:T(8,128)(2,1)}, bf16[4,128,512]{2,1,0:T(8,128)(2,1)S(1)}, u32[]{:S(2)}, u32[]{:S(2)}) collective-permute-start(bf16[4,128,512]{2,1,0:T(8,128)(2,1)} %param.15), channel_id=1, source_target_pairs={{16,0},{32,16},{48,32},{64,48},{80,64},{96,80},{112,96},{17,1},{33... | collective-permute-start | bytes 1572872 | tf_op jit(solution)/shard_map/ppermute | solution.py:447
  2.6 6.1 %pre_first.1 = (f32[2048,512]{1,0:T(8,128)}, bf16[512,512]{1,0:T(8,128)(2,1)}, s32[1,2048]{1,0:T(1,128)}, s32[1,2048]{1,0:T(1,128)}, bf16[2048,128]{1,0:T(8,128)(2,1)}) custom-call(bf16[2048,512]{1,0:T(8,128)(2,1)} %refs_3_.4, s32[1,2048]{1,0:T(1,128)} %refs_1_.5, bf16[128,512]{1,0:T(8,128)(2,1)} %refs_4_.1, bf16[3,3,512,512]{3,2,1,0:T(8,128)(2,1)} %refs_5_.5, ...), custom_call_target="tpu_custom_call" | custom-call | flops 1342177280 | bytes 6291456 | tf_op jit(solution)/shard_map/pre_first/pallas_call | solution.py:356
  8.8 0.8 fusion.1
  9.6 0.0 collective-permute-done
  9.6 0.0 collective-permute-done.1
  9.8 2.2 %collective-permute-start.2 = (bf16[48,512]{1,0:T(8,128)(2,1)S(1)}, bf16[48,512]{1,0:T(8,128)(2,1)S(1)}, u32[]{:S(2)}, u32[]{:S(2)}) collective-permute-start(bf16[48,512]{1,0:T(8,128)(2,1)S(1)} %reshape.30), channel_id=1, source_target_pairs={{0,1},{1,2},{2,3},{3,4},{4,5},{5,6},{6,7},{7,8},{8,9},{9,10},{10,1... | collective-permute-start | bytes 147464 | tf_op jit(solution)/shard_map/ppermute | solution.py:447
  12.0 5.0 %collective-permute-start.3 = (bf16[48,512]{1,0:T(8,128)(2,1)S(1)}, bf16[48,512]{1,0:T(8,128)(2,1)S(1)}, u32[]{:S(2)}, u32[]{:S(2)}) collective-permute-start(bf16[48,512]{1,0:T(8,128)(2,1)S(1)} %reshape.31), channel_id=1, source_target_pairs={{0,15},{1,0},{2,1},{3,2},{4,3},{5,4},{6,5},{7,6},{8,7},{9,8},{10,9... | collective-permute-start | bytes 147464 | tf_op jit(solution)/shard_map/ppermute | solution.py:447
  17.0 1.8 %halo_terms.1.refs_12_ = bf16[1024,512]{1,0:T(8,128)(2,1)S(1)} custom-call(bf16[512,512]{1,0:T(8,128)(2,1)S(1)} %bitcast.9, bf16[512,512]{1,0:T(8,128)(2,1)S(1)} %bitcast.10, bf16[3,3,512,512]{3,2,1,0:T(8,128)(2,1)} %refs_5_.5), custom_call_target="tpu_custom_call" | custom-call | flops 536870912 | bytes 1572864 | tf_op jit(solution)/shard_map/halo_terms/pallas_call | solution.py:375
  18.7 0.2 collective-permute-done.2.refs_13_
  19.0 0.0 collective-permute-done.3.refs_14_
  19.0 9.2 %encode.1 = (bf16[128,512]{1,0:T(8,128)(2,1)}, bf16[128,512]{1,0:T(8,128)(2,1)}, bf16[2048,512]{1,0:T(8,128)(2,1)}) custom-call(s32[1,2048]{1,0:T(1,128)} %get-tuple-element.21.refs_0_, s32[1,2048]{1,0:T(1,128)} %refs_1_.5, f32[2048,512]{1,0:T(8,128)} %get-tuple-element.22.refs_2_, bf16[2048,512]{1,0:T(8,128)(2,1)} %refs_3_.4, bf16[128,512]{1,0:T(8,128)(2,1)} %refs_4_.1, ...), custom_call_target="tpu_custom_call" | custom-call | flops 1342177280 | bytes 10485760 | tf_op jit(solution)/shard_map/encode/pallas_call | solution.py:428
  28.2 12.7 %all-to-all-start = ((bf16[128,16,512]{2,1,0:T(8,128)(2,1)}), bf16[128,16,512]{2,1,0:T(8,128)(2,1)S(1)}, u32[]{:S(2)}, u32[]{:S(2)}) async-start(bf16[128,16,512]{2,1,0:T(8,128)(2,1)} %bitcast.11), calls=%async_computation | async-start | bytes 4194304 | tf_op jit(solution)/shard_map/all_to_all | solution.py:495
  41.0 5.7 %pre_next.2.refs_2_ = f32[2048,512]{1,0:T(8,128)} custom-call(bf16[2048,512]{1,0:T(8,128)(2,1)} %refs_3_.5, s32[1,2048]{1,0:T(1,128)} %refs_1_.7, bf16[128,512]{1,0:T(8,128)(2,1)} %get-tuple-element.28.nodes_h.refs_4_, bf16[3,3,512,512]{3,2,1,0:T(8,128)(2,1)} %refs_5_.5), custom_call_target="tpu_custom_call" | custom-call | flops 1342177280 | bytes 6291456 | tf_op jit(solution)/shard_map/pre_next/pallas_call | solution.py:356
  46.7 23.9 %all-to-all-done = bf16[128,16,512]{2,1,0:T(8,128)(2,1)S(1)} async-done(((bf16[128,16,512]{2,1,0:T(8,128)(2,1)}), bf16[128,16,512]{2,1,0:T(8,128)(2,1)S(1)}, u32[]{:S(2)}, u32[]{:S(2)}) %all-to-all-start) | async-done | bytes 2097184 | tf_op jit(solution)/shard_map/all_to_all | solution.py:495
  70.6 9.1 %layer.2 = (bf16[128,512]{1,0:T(8,128)(2,1)}, bf16[128,512]{1,0:T(8,128)(2,1)}, bf16[2048,512]{1,0:T(8,128)(2,1)}, bf16[2048,512]{1,0:T(8,128)(2,1)}) custom-call(s32[1,2048]{1,0:T(1,128)} %get-tuple-element.20.refs_0_, s32[1,2048]{1,0:T(1,128)} %refs_1_.7, f32[2048,512]{1,0:T(8,128)} %pre_next.2.refs_2_, bf16[2048,512]{1,0:T(8,128)(2,1)} %refs_3_.5, ...), custom_call_target="tpu_custom_call" | custom-call | flops 1342177280 | bytes 10485760 | tf_op jit(solution)/shard_map/layer/pallas_call | solution.py:428
  79.7 4.7 %all-to-all-start.1 = ((bf16[128,16,512]{2,1,0:T(8,128)(2,1)}), bf16[128,16,512]{2,1,0:T(8,128)(2,1)S(1)}, u32[]{:S(2)}, u32[]{:S(2)}) async-start(bf16[128,16,512]{2,1,0:T(8,128)(2,1)} %bitcast.12), calls=%async_computation.1 | async-start | bytes 4194304 | tf_op jit(solution)/shard_map/all_to_all | solution.py:495
  84.3 5.7 %pre_next.3.refs_2_ = f32[2048,512]{1,0:T(8,128)} custom-call(bf16[2048,512]{1,0:T(8,128)(2,1)} %get-tuple-element.31.edges_h.refs_3_, s32[1,2048]{1,0:T(1,128)} %refs_1_.7, bf16[128,512]{1,0:T(8,128)(2,1)} %get-tuple-element.32.nodes_h.refs_4_, bf16[3,3,512,512]{3,2,1,0:T(8,128)(2,1)} %refs_5_.5), custom_call_target="tpu_custom_call" | custom-call | flops 1342177280 | bytes 6291456 | tf_op jit(solution)/shard_map/pre_next/pallas_call | solution.py:356
  90.0 24.1 %all-to-all-done.1 = bf16[128,16,512]{2,1,0:T(8,128)(2,1)S(1)} async-done(((bf16[128,16,512]{2,1,0:T(8,128)(2,1)}), bf16[128,16,512]{2,1,0:T(8,128)(2,1)S(1)}, u32[]{:S(2)}, u32[]{:S(2)}) %all-to-all-start.1) | async-done | bytes 2097184 | tf_op jit(solution)/shard_map/all_to_all | solution.py:495
  114.1 7.8 %layer.3 = bf16[128,512]{1,0:T(8,128)(2,1)} custom-call(s32[1,2048]{1,0:T(1,128)} %get-tuple-element.20.refs_0_, s32[1,2048]{1,0:T(1,128)} %refs_1_.7, f32[2048,512]{1,0:T(8,128)} %pre_next.3.refs_2_, bf16[2048,512]{1,0:T(8,128)(2,1)} %get-tuple-element.31.edges_h.refs_3_, bf16[128,512]{1,0:T(8,128)(2,1)} %get-tuple-element.32.nodes_h.refs_4_, ...), custom_call_target="tpu_custom_call" | custom-call | flops 1342177280 | bytes 10485760 | tf_op jit(solution)/shard_map/layer/pallas_call | solution.py:428
  (5 shorter events, 0.1 us)
Async XLA Ops:
  0.0 9.6 %collective-permute-start = (bf16[4,128,512]{2,1,0:T(8,128)(2,1)}, bf16[4,128,512]{2,1,0:T(8,128)(2,1)S(1)}, u32[]{:S(2)}, u32[]{:S(2)}) collective-permute-start(bf16[4,128,512]{2,1,0:T(8,128)(2,1)} %param.15), channel_id=1, source_target_pairs={{0,16},{16,32},{32,48},{48,64},{64,80},{80,96},{96,112},{1,17},{17... | collective-permute-start | bytes 1572872 | tf_op jit(solution)/shard_map/ppermute | solution.py:447
  1.3 8.3 %collective-permute-start.1 = (bf16[4,128,512]{2,1,0:T(8,128)(2,1)}, bf16[4,128,512]{2,1,0:T(8,128)(2,1)S(1)}, u32[]{:S(2)}, u32[]{:S(2)}) collective-permute-start(bf16[4,128,512]{2,1,0:T(8,128)(2,1)} %param.15), channel_id=1, source_target_pairs={{16,0},{32,16},{48,32},{64,48},{80,64},{96,80},{112,96},{17,1},{33... | collective-permute-start | bytes 1572872 | tf_op jit(solution)/shard_map/ppermute | solution.py:447
  9.8 9.2 %collective-permute-start.2 = (bf16[48,512]{1,0:T(8,128)(2,1)S(1)}, bf16[48,512]{1,0:T(8,128)(2,1)S(1)}, u32[]{:S(2)}, u32[]{:S(2)}) collective-permute-start(bf16[48,512]{1,0:T(8,128)(2,1)S(1)} %reshape.30), channel_id=1, source_target_pairs={{0,1},{1,2},{2,3},{3,4},{4,5},{5,6},{6,7},{7,8},{8,9},{9,10},{10,1... | collective-permute-start | bytes 147464 | tf_op jit(solution)/shard_map/ppermute | solution.py:447
  12.0 7.0 %collective-permute-start.3 = (bf16[48,512]{1,0:T(8,128)(2,1)S(1)}, bf16[48,512]{1,0:T(8,128)(2,1)S(1)}, u32[]{:S(2)}, u32[]{:S(2)}) collective-permute-start(bf16[48,512]{1,0:T(8,128)(2,1)S(1)} %reshape.31), channel_id=1, source_target_pairs={{0,15},{1,0},{2,1},{3,2},{4,3},{5,4},{6,5},{7,6},{8,7},{9,8},{10,9... | collective-permute-start | bytes 147464 | tf_op jit(solution)/shard_map/ppermute | solution.py:447
  28.2 42.3 %all-to-all-start = ((bf16[128,16,512]{2,1,0:T(8,128)(2,1)}), bf16[128,16,512]{2,1,0:T(8,128)(2,1)S(1)}, u32[]{:S(2)}, u32[]{:S(2)}) async-start(bf16[128,16,512]{2,1,0:T(8,128)(2,1)} %bitcast.11), calls=%async_computation | async-start | bytes 4194304 | tf_op jit(solution)/shard_map/all_to_all | solution.py:495
  79.7 34.4 %all-to-all-start.1 = ((bf16[128,16,512]{2,1,0:T(8,128)(2,1)}), bf16[128,16,512]{2,1,0:T(8,128)(2,1)S(1)}, u32[]{:S(2)}, u32[]{:S(2)}) async-start(bf16[128,16,512]{2,1,0:T(8,128)(2,1)} %bitcast.12), calls=%async_computation.1 | async-start | bytes 4194304 | tf_op jit(solution)/shard_map/all_to_all | solution.py:495
